TPU v7x, 32 devices: a whole 2x2x4 slice. The times are simulated.
32 devices in a mesh: dp: 4 (over x, core), mp: 8 (over z, y).
Axes of the slice: x: 2, y: 2, z: 4, core: 2. Of those that a mesh axis runs over, the one named last changes fastest.
Arguments:
- tokens: bfloat16 [128, 8192], P('dp', 'mp'), may hold values from -6 to 6
- gate_up_weight: bfloat16 [2, 8192, 15360], P(None, 'mp', 'dp'), may hold values from -0.0625 to 0.0625
- down_weight: bfloat16 [15360, 8192], P('dp', 'mp'), may hold values from -0.046875 to 0.046875
- gate_up_input_factor: bfloat16 [2, 8192, 64], P(None, 'mp'), may hold values from -0.0625 to 0.0625
- gate_up_output_factor: bfloat16 [2, 64, 15360], P(None, None, 'dp'), may hold values from -0.046875 to 0.046875
- down_input_factor: bfloat16 [15360, 64], P('dp'), may hold values from -0.046875 to 0.046875
- down_output_factor: bfloat16 [64, 8192], P(None, 'mp'), may hold values from -0.0625 to 0.0625
- cotangent: bfloat16 [128, 8192], P('dp', 'mp'), may hold values from -6 to 6
Outputs:
- output: bfloat16 [128, 8192], P('dp', 'mp')
- input_grad: bfloat16 [128, 8192], P('dp', 'mp')
- grad_gate_up_lower: float32 [2, 8192, 64], P(None, 'mp')
- gate_up_output_factor_gradient: float32 [2, 64, 15360], P(None, None, 'dp')
- down_input_factor_gradient: float32 [15360, 64], P('dp')
- down_output_factor_gradient: float32 [64, 8192], P(None, 'mp')
All inputs are finite; a program needn't handle non-finite values.
Results may differ from a plain program's by a relative error of at most 0.0065.
Values may be sent and summed in bfloat16 or wider, within the bound.
No kernel may reach another device: no remote copies, remote signals or barrier semaphores. Data moves between devices by JAX's collectives and lax.ppermute only.
A program may use at most 64 MiB of HBM per device.

v0:
```python
import jax
import jax.numpy as jnp
from jax import lax
from jax.experimental import pallas as pl
from jax.experimental.pallas import tpu as pltpu
from jax.sharding import PartitionSpec as P


adapter_scale = 2.0
single = jnp.float32
half = jnp.bfloat16
HIGHEST = lax.Precision.HIGHEST
vmem_limit = 30 * 2**20
load_limit = 38 * 2**20


def dot(left, right, dims=((1,), (0,)), precision=None):
    return lax.dot_general(
        left, right, (dims, ((), ())), preferred_element_type=single, precision=precision
    )


def exchange(value, axis, mask):
    size = lax.axis_size(axis)
    return lax.ppermute(value, axis, [(i, i ^ mask) for i in range(size)])


def mp_mask(position, size):
    rest = size // 4
    return (position // rest) | ((position % rest) << 2)


def dp_mask(position, size):
    mask, bits = 0, size.bit_length() - 1
    for bit in range(bits):
        mask = mask | (((position >> (bits - 1 - bit)) & 1) << bit)
    return mask


def owners(axis, total, mask_of):
    size = lax.axis_size(axis)
    rows = total // size
    row = lax.iota(jnp.int32, total)
    block = row // rows
    return (lax.axis_index(axis) ^ mask_of(block, size)) * rows + row % rows


def tile(size, limit):
    return max(t for t in range(128, limit + 1, 128) if size % t == 0)


def load(down_weight, gate_up_weight):
    rows, width = down_weight.shape
    depth = gate_up_weight.shape[1]
    parts = 8

    def kernel(down_ref, wide_ref, down_out, gate_out, done):
        copies = []
        for i in range(parts):
            span = pl.ds(i * (rows // parts), rows // parts)
            copies.append(
                pltpu.make_async_copy(down_ref.at[span], down_out.at[span], done.at[0, i])
            )
        for i in range(parts):
            span = pl.ds(i * (depth // parts), depth // parts)
            copies.append(
                pltpu.make_async_copy(wide_ref.at[0, span], gate_out.at[span], done.at[1, i])
            )
        for copy in copies:
            copy.start()
        for copy in copies:
            copy.wait()

    anywhere = pl.BlockSpec(memory_space=pl.ANY)
    return pl.pallas_call(
        kernel,
        in_specs=[anywhere] * 2,
        out_specs=[anywhere] * 2,
        out_shape=[
            jax.ShapeDtypeStruct(down_weight.shape, half),
            jax.ShapeDtypeStruct(gate_up_weight.shape[1:], half),
        ],
        scratch_shapes=[pltpu.SemaphoreType.DMA((2, parts))],
        cost_estimate=pl.CostEstimate(
            flops=10**10, bytes_accessed=4 * rows * (width + depth), transcendentals=0
        ),
        compiler_params=pltpu.CompilerParams(vmem_limit_bytes=load_limit),
    )(down_weight, gate_up_weight)


def project(x, cot, to_true, gate_weight, weight, input_factor, output_factor, hidden):
    total, depth = x.shape
    step = tile(hidden, 768)
    count = hidden // step
    quarter = total // 4
    rows = quarter // 2
    rank = output_factor.shape[0]

    def kernel(*refs):
        x_ref, cot_ref, true_ref, gate_ref, w_ref, in_ref, out_ref = refs[:7]
        near, far, (keep_near, keep_far, low, held, done) = refs[7:10], refs[10:13], refs[13:]

        def fetch(i):
            return pltpu.make_async_copy(
                w_ref.at[1, :, pl.ds(i * step, step)], held.at[i], done.at[i]
            )

        for i in range(count):
            fetch(i).start()
        over = ((1,), (1,))
        parts = [dot(cot_ref[...], out_ref[...], over)]
        parts += [dot(x_ref[...], in_ref[k], over) for k in range(2)]
        for k in range(3):
            low[:, k * rank : (k + 1) * rank] = dot(
                true_ref[...], parts[k].astype(half)
            ).astype(half)
        for i in range(2 * count):
            if i < count:
                block = gate_ref[:, i * step : (i + 1) * step]
            else:
                fetch(i - count).wait()
                block = held[i - count]
            acc = dot(x_ref[...], block)
            span = slice(i * step, (i + 1) * step)
            keep_near[:, span] = acc[:rows]
            keep_far[:, span] = acc[rows:quarter]
            for m in range(1, 4):
                first = acc[m * quarter : m * quarter + rows]
                second = acc[m * quarter + rows : (m + 1) * quarter]
                near[m - 1][:, span] = first.astype(half)
                far[m - 1][:, span] = second.astype(half)

    shape = lambda kind: jax.ShapeDtypeStruct((rows, 2 * hidden), kind)
    vmem = pl.BlockSpec(memory_space=pltpu.VMEM)
    out = pl.pallas_call(
        kernel,
        in_specs=[vmem] * 4 + [pl.BlockSpec(memory_space=pl.ANY)] + [vmem] * 2,
        out_specs=[vmem] * 9,
        out_shape=[shape(half)] * 6
        + [shape(single)] * 2
        + [jax.ShapeDtypeStruct((total, 3 * rank), half)],
        scratch_shapes=[pltpu.VMEM((count, depth, step), half), pltpu.SemaphoreType.DMA((count,))],
        cost_estimate=pl.CostEstimate(
            flops=16 * total * depth * hidden,
            bytes_accessed=4 * depth * hidden,
            transcendentals=0,
        ),
        compiler_params=pltpu.CompilerParams(vmem_limit_bytes=vmem_limit),
    )(x, cot, to_true, gate_weight, weight, input_factor, output_factor)
    return out[:3], out[3:6], out[6], out[7], out[8]


def near_sum(keep, sends):
    got = [exchange(sends[m - 1], "mp", m) for m in (3, 2, 1)]
    return [keep] + [piece.astype(single) for piece in got]


def far_rest(total, rest):
    rows = total.shape[0] // rest
    while rest > 1:
        rest //= 2
        piece = exchange(total[rest * rows :].astype(half), "mp", rest << 2)
        total = total[: rest * rows] + piece.astype(single)
    return total


def gather_rest(block):
    size = lax.axis_size("mp")
    step = 1
    while step < size // 8:
        block = jnp.concatenate([block, exchange(block, "mp", step << 2)], axis=0)
        step *= 2
    return block


def gather_near(block):
    got = {m: exchange(block, "mp", m) for m in (3, 2, 1)}
    return [block] + [got[m] for m in (1, 2, 3)]


def weave(near, far):
    return jnp.concatenate([part for pair in zip(near, far) for part in pair], axis=0)


def scatter_dp(partial):
    size = lax.axis_size("dp")
    bit = 1
    while bit < size:
        count = partial.shape[0] // 2
        piece = partial[count:].astype(half)
        piece = exchange(piece, "dp", bit)
        partial = partial[:count] + piece.astype(single)
        bit *= 2
    return partial


def sum_all(partial, axis):
    size = lax.axis_size(axis)
    bit = 1
    while bit < size:
        rounded = partial.astype(half)
        partial = rounded.astype(single) + exchange(rounded, axis, bit).astype(single)
        bit *= 2
    return partial


def per_device(
    tokens,
    gate_up_weight,
    down_weight,
    gate_up_input_factor,
    gate_up_output_factor,
    down_input_factor,
    down_output_factor,
    cotangent,
):
    own, _ = tokens.shape
    hidden_width, rank = down_input_factor.shape
    block = jnp.concatenate([tokens, cotangent], axis=0)
    dp_size = lax.axis_size("dp")
    pieces = [block] + [exchange(block, "dp", m) for m in range(1, dp_size)]
    down_weight, gate_weight = load(down_weight, gate_up_weight)
    both = jnp.concatenate(pieces, axis=0)
    total = both.shape[0] // 2
    gradient_scale = adapter_scale * total ** (-0.5)
    mp_token = owners("mp", total, mp_mask)
    dp_token = owners("dp", total, dp_mask)
    order = lax.iota(jnp.int32, total)
    row = lax.iota(jnp.int32, 2 * total)
    got_token = (lax.axis_index("dp") ^ (row // (2 * own))) * own + row % own
    got_kind = row // own % 2
    match = mp_token[:, None] == got_token[None, :]
    to_mp = jnp.concatenate(
        [match & (got_kind == kind)[None, :] for kind in range(2)], axis=0
    ).astype(half)
    to_true = (order[:, None] == mp_token[None, :]).astype(half)
    from_true = (mp_token[:, None] == order[None, :]).astype(half)
    to_dp = (dp_token[:, None] == mp_token[None, :]).astype(single)
    own_dp = (dp_token[:own, None] == order[None, :]).astype(single)
    both = dot(to_mp, both).astype(half)
    x = both[:total]
    cot = both[total:]

    back_part = dot(cot, down_weight, ((1,), (1,)))
    quarter = total // 4
    back_sends = [
        back_part[m * quarter : (m + 1) * quarter].astype(half) for m in (1, 2, 3)
    ]
    pre_near, pre_far, pre_near_keep, pre_far_keep, low_part = project(
        x,
        cot,
        to_true,
        gate_weight,
        gate_up_weight,
        jnp.swapaxes(gate_up_input_factor, 1, 2),
        down_output_factor,
        hidden_width,
    )
    low_sum = sum_all(low_part, "mp").astype(half)
    low_sum = dot(from_true, low_sum).astype(half)
    back_down_all = low_sum[:, :rank]
    low_all = [low_sum[:, (k + 1) * rank : (k + 2) * rank] for k in range(2)]

    size = lax.axis_size("mp")
    top = size // 2
    back_parts = near_sum(back_part[:quarter], back_sends)
    pre_parts = near_sum(pre_far_keep, pre_far)
    back_total = sum(back_parts)
    back_crossed = back_total[quarter // 2 :].astype(half)
    pre_crossed = sum(pre_parts).astype(half)
    back_crossed = exchange(back_crossed, "mp", top)
    pre_crossed = exchange(pre_crossed, "mp", top)
    back_own = back_total[: quarter // 2] + back_crossed.astype(single)
    pre_own = sum(near_sum(pre_near_keep, pre_near)) + pre_crossed.astype(single)
    back_own = far_rest(back_own, size // 8)
    pre_own = far_rest(pre_own, size // 8)

    rows = pre_own.shape[0]
    gate, up = [
        pre_own[:, k * hidden_width : (k + 1) * hidden_width]
        + adapter_scale * dot(low_all[k][:rows], gate_up_output_factor[k])
        for k in range(2)
    ]
    hidden = (jax.nn.silu(gate) * up).astype(half)
    hidden_back = back_own + adapter_scale * dot(
        back_down_all[:rows], down_input_factor, ((1,), (1,))
    )
    sigma = jax.nn.sigmoid(gate)
    gate_back = (hidden_back * up * sigma * (1.0 + gate * (1.0 - sigma))).astype(half)
    up_back = (hidden_back * gate * sigma).astype(half)

    block = gather_rest(jnp.concatenate([hidden, gate_back, up_back], axis=1))
    crossed = exchange(block, "mp", top)
    near_block = gather_near(block)
    crossed, near_block[1] = lax.optimization_barrier((crossed, near_block[1]))
    far_hidden = gather_near(crossed[:, :hidden_width])
    far_back = gather_near(crossed[:, hidden_width:])
    hidden_all = weave([piece[:, :hidden_width] for piece in near_block], far_hidden)
    back_all = weave([piece[:, hidden_width:] for piece in near_block], far_back)
    back_all = [back_all[:, k * hidden_width : (k + 1) * hidden_width] for k in range(2)]

    low_down = sum_all(dot(hidden_all, down_input_factor), "dp")
    output_own = scatter_dp(dot(to_dp, dot(hidden_all, down_weight), precision=HIGHEST))
    down_input_factor_gradient = gradient_scale * dot(hidden_all, back_down_all, ((0,), (0,)))
    low_down_own = dot(to_dp[:own], low_down, precision=HIGHEST)
    output = output_own + adapter_scale * dot(
        low_down_own, down_output_factor.astype(single), precision=HIGHEST
    )
    down_output_factor_gradient = gradient_scale * dot(
        low_down, cot.astype(single), ((0,), (0,)), HIGHEST
    )

    gate_up_output_factor_gradient = gradient_scale * jnp.stack(
        [dot(low_all[k], back_all[k], ((0,), (0,))) for k in range(2)]
    )
    back_low = sum_all(
        jnp.concatenate(
            [dot(back_all[k], gate_up_output_factor[k], ((1,), (1,))) for k in range(2)], axis=1
        ),
        "dp",
    ).astype(half)
    grad_gate_up_lower = gradient_scale * jnp.stack(
        [dot(x, back_low[:, k * rank : (k + 1) * rank], ((0,), (0,))) for k in range(2)]
    )
    grad_part = dot(back_all[0], gate_up_weight[0], ((1,), (1,)))
    grad_part = grad_part + dot(back_all[1], gate_up_weight[1], ((1,), (1,)))
    grad_own = scatter_dp(dot(to_dp, grad_part, precision=HIGHEST))
    back_low_own = dot(to_dp[:own].astype(half), back_low).astype(half)
    for k in range(2):
        grad_own = grad_own + adapter_scale * dot(
            back_low_own[:, k * rank : (k + 1) * rank], gate_up_input_factor[k], ((1,), (1,))
        )
    return (
        output.astype(half),
        grad_own.astype(half),
        grad_gate_up_lower,
        gate_up_output_factor_gradient,
        down_input_factor_gradient,
        down_output_factor_gradient,
    )


def solution(mesh):
    placed = (
        P("dp", "mp"),
        P(None, "mp", "dp"),
        P("dp", "mp"),
        P(None, "mp", None),
        P(None, None, "dp"),
        P("dp", None),
        P(None, "mp"),
        P("dp", "mp"),
    )

    return jax.shard_map(
        per_device,
        mesh=mesh,
        in_specs=placed,
        out_specs=(
            P("dp", "mp"),
            P("dp", "mp"),
            P(None, "mp", None),
            P(None, None, "dp"),
            P("dp", None),
            P(None, "mp"),
        ),
        check_vma=False,
    )
```

profile of v0, /device:TPU:0, one launch (start us, length us, event | category | flops | bytes accessed | tf_op | source)
XLA Modules:
  0.0 149.7 jit_solution(4428409735466348009)
XLA Ops:
  0.6 0.9 constant_dynamic-update-slice_fusion.1
  1.6 0.9 constant_dynamic-update-slice_fusion
  2.4 2.5 %collective-permute-start.2 = (bf16[64,1024]{1,0:T(8,128)(2,1)S(1)}, bf16[64,1024]{1,0:T(8,128)(2,1)S(1)}, u32[]{:S(2)}, u32[]{:S(2)}) collective-permute-start(bf16[64,1024]{1,0:T(8,128)(2,1)S(1)} %get-tuple-element.45), channel_id=1, source_target_pairs={{0,24},{8,16},{16,8},{24,0},{1,25},{9,17},{17,9},{25,1},{2,26},{10... | collective-permute-start | bytes 393224 | tf_op jit(solution)/shard_map/ppermute | solution.py:25
  5.6 5.8 %shard_map.127 = (bf16[3840,1024]{1,0:T(8,128)(2,1)S(1)}, bf16[1024,3840]{1,0:T(8,128)(2,1)S(1)}) custom-call(bf16[3840,1024]{1,0:T(8,128)(2,1)} %down_ref.1, bf16[2,1024,3840]{2,1,0:T(8,128)(2,1)} %refs_4_.1), custom_call_target="tpu_custom_call" | custom-call | flops 10000000000 | bytes 31457280 | tf_op jit(solution)/shard_map/pallas_call | solution.py:75
  12.4 4.1 %shard_map.128 = (bf16[16,7680]{1,0:T(8,128)(2,1)S(1)}, bf16[16,7680]{1,0:T(8,128)(2,1)S(1)}, bf16[16,7680]{1,0:T(8,128)(2,1)S(1)}, bf16[16,7680]{1,0:T(8,128)(2...) custom-call(bf16[128,1024]{1,0:T(8,128)(2,1)S(1)} %get-tuple-element, ...), custom_call_target="tpu_custom_call" | custom-call | flops 8053063680 | bytes 15728640 | tf_op jit(solution)/shard_map/pallas_call | solution.py:135
  16.5 2.2 %collective-permute-start.10 = (bf16[128,192]{1,0:T(8,128)(2,1)S(1)}, bf16[128,192]{1,0:T(8,128)(2,1)S(1)}, u32[]{:S(2)}, u32[]{:S(2)}) collective-permute-start(bf16[128,192]{1,0:T(8,128)(2,1)S(1)} %get-tuple-element.28), channel_id=1, source_target_pairs={{0,1},{1,0},{2,3},{3,2},{4,5},{5,4},{6,7},{7,6},{8,9},{9,8},{10,11... | collective-permute-start | bytes 147464 | tf_op jit(solution)/shard_map/ppermute | solution.py:25
  18.7 1.5 %collective-permute-start.3 = (bf16[16,7680]{1,0:T(8,128)(2,1)S(1)}, bf16[16,7680]{1,0:T(8,128)(2,1)S(1)}, u32[]{:S(2)}, u32[]{:S(2)}) collective-permute-start(bf16[16,7680]{1,0:T(8,128)(2,1)S(1)} %get-tuple-element.21), channel_id=1, source_target_pairs={{0,3},{1,2},{2,1},{3,0},{4,7},{5,6},{6,5},{7,4},{8,11},{9,10},{10,... | collective-permute-start | bytes 737288 | tf_op jit(solution)/shard_map/ppermute | solution.py:25
  20.3 2.9 %collective-permute-start.6 = (bf16[16,7680]{1,0:T(8,128)(2,1)S(1)}, bf16[16,7680]{1,0:T(8,128)(2,1)S(1)}, u32[]{:S(2)}, u32[]{:S(2)}) collective-permute-start(bf16[16,7680]{1,0:T(8,128)(2,1)S(1)} %get-tuple-element.25), channel_id=1, source_target_pairs={{0,3},{1,2},{2,1},{3,0},{4,7},{5,6},{6,5},{7,4},{8,11},{9,10},{10,... | collective-permute-start | bytes 737288 | tf_op jit(solution)/shard_map/ppermute | solution.py:25
  23.6 1.6 %collective-permute-done.10 = bf16[128,192]{1,0:T(8,128)(2,1)S(1)} collective-permute-done((bf16[128,192]{1,0:T(8,128)(2,1)S(1)}, bf16[128,192]{1,0:T(8,128)(2,1)S(1)}, u32[]{:S(2)}, u32[]{:S(2)}) %collective-permute-start.10) | collective-permute-done | bytes 49184 | tf_op jit(solution)/shard_map/ppermute | solution.py:25
  25.3 1.3 collective-permute-start.11
  26.6 2.7 %fusion.84 = (bf16[128,3840]{1,0:T(8,128)(2,1)S(1)}, f32[128,3840]{1,0:T(8,128)S(1)}) fusion(bf16[3840,1024]{1,0:T(8,128)(2,1)S(1)} %get-tuple-element.29, bf16[256,1024]{1,0:T(8,128)(2,1)S(1)} %convolution_convert_fusion), kind=kOutput, calls=%fused_computation.181 | convolution fusion | flops 1007124480 | bytes 11075584 | tf_op jit(solution)/shard_map/dot_general | solution.py:18
  29.3 14.1 %collective-permute-done.11 = bf16[128,192]{1,0:T(8,128)(2,1)S(1)} collective-permute-done((bf16[128,192]{1,0:T(8,128)(2,1)S(1)}, bf16[128,192]{1,0:T(8,128)(2,1)S(1)}, u32[]{:S(2)}, u32[]{:S(2)}) %collective-permute-start.11) | collective-permute-done | bytes 49184 | tf_op jit(solution)/shard_map/ppermute | solution.py:25
  43.4 2.8 %collective-permute-start.12 = (bf16[128,192]{1,0:T(8,128)(2,1)S(1)}, bf16[128,192]{1,0:T(8,128)(2,1)S(1)}, u32[]{:S(2)}, u32[]{:S(2)}) collective-permute-start(bf16[128,192]{1,0:T(8,128)(2,1)S(1)} %add_convert_fusion.2), channel_id=1, source_target_pairs={{0,4},{1,5},{2,6},{3,7},{4,0},{5,1},{6,2},{7,3},{8,12},{9,13},{10,... | collective-permute-start | bytes 147464 | tf_op jit(solution)/shard_map/ppermute | solution.py:25
  46.3 2.4 %collective-permute-done.12 = bf16[128,192]{1,0:T(8,128)(2,1)S(1)} collective-permute-done((bf16[128,192]{1,0:T(8,128)(2,1)S(1)}, bf16[128,192]{1,0:T(8,128)(2,1)S(1)}, u32[]{:S(2)}, u32[]{:S(2)}) %collective-permute-start.12) | collective-permute-done | bytes 49184 | tf_op jit(solution)/shard_map/ppermute | solution.py:25
  48.7 1.6 %collective-permute-start.8 = (bf16[16,7680]{1,0:T(8,128)(2,1)S(1)}, bf16[16,7680]{1,0:T(8,128)(2,1)S(1)}, u32[]{:S(2)}, u32[]{:S(2)}) collective-permute-start(bf16[16,7680]{1,0:T(8,128)(2,1)S(1)} %get-tuple-element.27), channel_id=1, source_target_pairs={{0,1},{1,0},{2,3},{3,2},{4,5},{5,4},{6,7},{7,6},{8,9},{9,8},{10,11... | collective-permute-start | bytes 737288 | tf_op jit(solution)/shard_map/ppermute | solution.py:25
  50.8 1.6 %collective-permute-start.13 = (bf16[32,3840]{1,0:T(8,128)(2,1)S(1)}, bf16[32,3840]{1,0:T(8,128)(2,1)S(1)}, u32[]{:S(2)}, u32[]{:S(2)}) collective-permute-start(bf16[32,3840]{1,0:T(8,128)(2,1)S(1)} %get-tuple-element.36), channel_id=1, source_target_pairs={{0,3},{1,2},{2,1},{3,0},{4,7},{5,6},{6,5},{7,4},{8,11},{9,10},{10,... | collective-permute-start | bytes 737288 | tf_op jit(solution)/shard_map/ppermute | solution.py:25
  52.4 1.5 collective-permute-start.15
  53.9 8.6 %collective-permute-done.8 = bf16[16,7680]{1,0:T(8,128)(2,1)S(1)} collective-permute-done((bf16[16,7680]{1,0:T(8,128)(2,1)S(1)}, bf16[16,7680]{1,0:T(8,128)(2,1)S(1)}, u32[]{:S(2)}, u32[]{:S(2)}) %collective-permute-start.8) | collective-permute-done | bytes 245792 | tf_op jit(solution)/shard_map/ppermute | solution.py:25
  62.5 1.7 %collective-permute-start.14 = (bf16[32,3840]{1,0:T(8,128)(2,1)S(1)}, bf16[32,3840]{1,0:T(8,128)(2,1)S(1)}, u32[]{:S(2)}, u32[]{:S(2)}) collective-permute-start(bf16[32,3840]{1,0:T(8,128)(2,1)S(1)} %get-tuple-element.38), channel_id=1, source_target_pairs={{0,2},{1,3},{2,0},{3,1},{4,6},{5,7},{6,4},{7,5},{8,10},{9,11},{10,... | collective-permute-start | bytes 737288 | tf_op jit(solution)/shard_map/ppermute | solution.py:25
  64.9 2.8 %collective-permute-done.15 = bf16[32,3840]{1,0:T(8,128)(2,1)S(1)} collective-permute-done((bf16[32,3840]{1,0:T(8,128)(2,1)S(1)}, bf16[32,3840]{1,0:T(8,128)(2,1)S(1)}, u32[]{:S(2)}, u32[]{:S(2)}) %collective-permute-start.15) | collective-permute-done | bytes 245792 | tf_op jit(solution)/shard_map/ppermute | solution.py:25
  67.7 2.5 %collective-permute-start.9 = (bf16[16,7680]{1,0:T(8,128)(2,1)S(1)}, bf16[16,7680]{1,0:T(8,128)(2,1)S(1)}, u32[]{:S(2)}, u32[]{:S(2)}) collective-permute-start(bf16[16,7680]{1,0:T(8,128)(2,1)S(1)} %add_convert_fusion), channel_id=1, source_target_pairs={{0,4},{1,5},{2,6},{3,7},{4,0},{5,1},{6,2},{7,3},{8,12},{9,13},{10,... | collective-permute-start | bytes 737288 | tf_op jit(solution)/shard_map/ppermute | solution.py:25
  70.2 1.4 collective-permute-done.14
  71.7 2.5 %collective-permute-start.16 = (bf16[16,3840]{1,0:T(8,128)(2,1)S(1)}, bf16[16,3840]{1,0:T(8,128)(2,1)S(1)}, u32[]{:S(2)}, u32[]{:S(2)}) collective-permute-start(bf16[16,3840]{1,0:T(8,128)(2,1)S(1)} %slice.362), channel_id=1, source_target_pairs={{0,4},{1,5},{2,6},{3,7},{4,0},{5,1},{6,2},{7,3},{8,12},{9,13},{10,... | collective-permute-start | bytes 368648 | tf_op jit(solution)/shard_map/ppermute | solution.py:25
  74.2 6.4 %collective-permute-done.9 = bf16[16,7680]{1,0:T(8,128)(2,1)S(1)} collective-permute-done((bf16[16,7680]{1,0:T(8,128)(2,1)S(1)}, bf16[16,7680]{1,0:T(8,128)(2,1)S(1)}, u32[]{:S(2)}, u32[]{:S(2)}) %collective-permute-start.9) | collective-permute-done | bytes 245792 | tf_op jit(solution)/shard_map/ppermute | solution.py:25
  81.3 0.7 collective-permute-done.16
  82.2 2.3 %collective-permute-start.22 = (bf16[16,11520]{1,0:T(8,128)(2,1)S(1)}, bf16[16,11520]{1,0:T(8,128)(2,1)S(1)}, u32[]{:S(2)}, u32[]{:S(2)}) collective-permute-start(bf16[16,11520]{1,0:T(8,128)(2,1)S(1)} %pad_maximum_fusion), channel_id=1, source_target_pairs={{0,3},{1,2},{2,1},{3,0},{4,7},{5,6},{6,5},{7,4},{8,11},{9,10},{10,... | collective-permute-start | bytes 1105928 | tf_op jit(solution)/shard_map/ppermute | solution.py:25
  84.5 1.1 collective-permute-start.20
  85.7 2.8 %collective-permute-start.17 = (bf16[16,11520]{1,0:T(8,128)(2,1)S(1)}, bf16[16,11520]{1,0:T(8,128)(2,1)S(1)}, u32[]{:S(2)}, u32[]{:S(2)}) collective-permute-start(bf16[16,11520]{1,0:T(8,128)(2,1)S(1)} %pad_maximum_fusion), channel_id=1, source_target_pairs={{0,4},{1,5},{2,6},{3,7},{4,0},{5,1},{6,2},{7,3},{8,12},{9,13},{10,... | collective-permute-start | bytes 1105928 | tf_op jit(solution)/shard_map/ppermute | solution.py:25
  88.6 8.2 %collective-permute-done.18 = bf16[16,11520]{1,0:T(8,128)(2,1)S(1)} collective-permute-done((bf16[16,11520]{1,0:T(8,128)(2,1)S(1)}, bf16[16,11520]{1,0:T(8,128)(2,1)S(1)}, u32[]{:S(2)}, u32[]{:S(2)}) %collective-permute-start.18) | collective-permute-done | bytes 368672 | tf_op jit(solution)/shard_map/ppermute | solution.py:25
  96.8 10.8 %collective-permute-done.17 = bf16[16,11520]{1,0:T(8,128)(2,1)S(1)} collective-permute-done((bf16[16,11520]{1,0:T(8,128)(2,1)S(1)}, bf16[16,11520]{1,0:T(8,128)(2,1)S(1)}, u32[]{:S(2)}, u32[]{:S(2)}) %collective-permute-start.17) | collective-permute-done | bytes 368672 | tf_op jit(solution)/shard_map/ppermute | solution.py:25
  107.6 4.2 %collective-permute-start.23 = (bf16[16,3840]{1,0:T(8,128)(2,1)S(1)}, bf16[16,3840]{1,0:T(8,128)(2,1)S(1)}, u32[]{:S(2)}, u32[]{:S(2)}) collective-permute-start(bf16[16,3840]{1,0:T(8,128)(2,1)S(1)} %get-tuple-element.43), channel_id=1, source_target_pairs={{0,3},{1,2},{2,1},{3,0},{4,7},{5,6},{6,5},{7,4},{8,11},{9,10},{10,... | collective-permute-start | bytes 368648 | tf_op jit(solution)/shard_map/ppermute | solution.py:25
  112.5 4.1 %collective-permute-done.19 = bf16[16,3840]{1,0:T(8,128)(2,1)S(1)} collective-permute-done((bf16[16,3840]{1,0:T(8,128)(2,1)S(1)}, bf16[16,3840]{1,0:T(8,128)(2,1)S(1)}, u32[]{:S(2)}, u32[]{:S(2)}) %collective-permute-start.19) | collective-permute-done | bytes 122912 | tf_op jit(solution)/shard_map/ppermute | solution.py:25
  116.6 2.5 %collective-permute-start.30 = (bf16[16,7680]{1,0:T(8,128)(2,1)S(1)}, bf16[16,7680]{1,0:T(8,128)(2,1)S(1)}, u32[]{:S(2)}, u32[]{:S(2)}) collective-permute-start(bf16[16,7680]{1,0:T(8,128)(2,1)S(1)} %get-tuple-element.41), channel_id=1, source_target_pairs={{0,3},{1,2},{2,1},{3,0},{4,7},{5,6},{6,5},{7,4},{8,11},{9,10},{10,... | collective-permute-start | bytes 737288 | tf_op jit(solution)/shard_map/ppermute | solution.py:25
  119.2 1.1 collective-permute-start.28
  120.4 1.2 fusion.85
  122.1 1.2 convolution_multiply_fusion
  123.4 1.6 %collective-permute-start.27 = (bf16[128,64]{0,1:T(8,128)(2,1)S(1)}, bf16[128,64]{0,1:T(8,128)(2,1)S(1)}, u32[]{:S(2)}, u32[]{:S(2)}) collective-permute-start(bf16[128,64]{0,1:T(8,128)(2,1)S(1)} %add_convert_fusion.7), channel_id=1, source_target_pairs={{0,16},{8,24},{16,0},{24,8},{1,17},{9,25},{17,1},{25,9},{2,18},{10... | collective-permute-start | bytes 49160 | tf_op jit(solution)/shard_map/ppermute | solution.py:25
  125.7 1.5 collective-permute-done.27
  127.6 1.0 convolution_multiply_fusion.4
  128.6 0.7 collective-permute-done.28
  130.4 2.8 %fusion = f32[128,1024]{1,0:T(8,128)S(1)} fusion(bf16[2,1024,3840]{2,1,0:T(8,128)(2,1)S(1)} %bitcast.54, bf16[128,7680]{1,0:T(8,128)(2,1)S(1)} %constant_dynamic-update-slice_fusion.12), kind=kOutput, calls=%fused_computation | convolution fusion | flops 1006632960 | bytes 9371648 | tf_op jit(solution)/shard_map/dot_general | solution.py:18
  133.8 2.6 %fusion.6 = f32[128,1024]{1,0:T(8,128)S(1)} fusion(f32[128,1024]{1,0:T(8,128)S(1)} %fusion, bf16[2,1024,3840]{2,1,0:T(8,128)(2,1)S(1)} %bitcast.54, bf16[128,7680]{1,0:T(8,128)(2,1)S(1)} %constant_dynamic-update-slice_fusion.12), kind=kOutput, calls=%fused_computation.14 | convolution fusion | flops 1006764032 | bytes 9895936 | tf_op jit(solution)/shard_map/dot_general | solution.py:18
  137.4 1.4 maximum_multiply_fusion
  138.9 1.6 %collective-permute-start.34 = (bf16[128,128]{0,1:T(8,128)(2,1)S(1)}, bf16[128,128]{0,1:T(8,128)(2,1)S(1)}, u32[]{:S(2)}, u32[]{:S(2)}) collective-permute-start(bf16[128,128]{0,1:T(8,128)(2,1)S(1)} %add_convert_fusion.6), channel_id=1, source_target_pairs={{0,16},{8,24},{16,0},{24,8},{1,17},{9,25},{17,1},{25,9},{2,18},{10... | collective-permute-start | bytes 98312 | tf_op jit(solution)/shard_map/ppermute | solution.py:25
  141.1 1.8 %collective-permute-done.34 = bf16[128,128]{0,1:T(8,128)(2,1)S(1)} collective-permute-done((bf16[128,128]{0,1:T(8,128)(2,1)S(1)}, bf16[128,128]{0,1:T(8,128)(2,1)S(1)}, u32[]{:S(2)}, u32[]{:S(2)}) %collective-permute-start.34) | collective-permute-done | bytes 32800 | tf_op jit(solution)/shard_map/ppermute | solution.py:25
  143.8 0.8 maximum_multiply_fusion.1
  144.7 1.7 %collective-permute-start.32 = (bf16[32,1024]{1,0:T(8,128)(2,1)S(1)}, bf16[32,1024]{1,0:T(8,128)(2,1)S(1)}, u32[]{:S(2)}, u32[]{:S(2)}) collective-permute-start(bf16[32,1024]{1,0:T(8,128)(2,1)S(1)} %slice.363), channel_id=1, source_target_pairs={{0,16},{8,24},{16,0},{24,8},{1,17},{9,25},{17,1},{25,9},{2,18},{10... | collective-permute-start | bytes 196616 | tf_op jit(solution)/shard_map/ppermute | solution.py:25
  147.0 2.0 %collective-permute-done.32 = bf16[32,1024]{1,0:T(8,128)(2,1)S(1)} collective-permute-done((bf16[32,1024]{1,0:T(8,128)(2,1)S(1)}, bf16[32,1024]{1,0:T(8,128)(2,1)S(1)}, u32[]{:S(2)}, u32[]{:S(2)}) %collective-permute-start.32) | collective-permute-done | bytes 65568 | tf_op jit(solution)/shard_map/ppermute | solution.py:25
  (115 shorter events, 12.5 us)
Async XLA Ops:
  0.6 49.9 %copy-start = (bf16[3840,64]{0,1:T(8,128)(2,1)S(1)}, bf16[3840,64]{0,1:T(8,128)(2,1)}, u32[]{:S(2)}) copy-start(bf16[3840,64]{0,1:T(8,128)(2,1)} %param.13) | copy-start | bytes 1474564
  2.4 9.4 %collective-permute-start.2 = (bf16[64,1024]{1,0:T(8,128)(2,1)S(1)}, bf16[64,1024]{1,0:T(8,128)(2,1)S(1)}, u32[]{:S(2)}, u32[]{:S(2)}) collective-permute-start(bf16[64,1024]{1,0:T(8,128)(2,1)S(1)} %get-tuple-element.45), channel_id=1, source_target_pairs={{0,24},{8,16},{16,8},{24,0},{1,25},{9,17},{17,9},{25,1},{2,26},{10... | collective-permute-start | bytes 393224 | tf_op jit(solution)/shard_map/ppermute | solution.py:25
  4.9 6.9 %collective-permute-start.1 = (bf16[64,1024]{1,0:T(8,128)(2,1)S(1)}, bf16[64,1024]{1,0:T(8,128)(2,1)S(1)}, u32[]{:S(2)}, u32[]{:S(2)}) collective-permute-start(bf16[64,1024]{1,0:T(8,128)(2,1)S(1)} %get-tuple-element.45), channel_id=1, source_target_pairs={{0,16},{8,24},{16,0},{24,8},{1,17},{9,25},{17,1},{25,9},{2,18},{10... | collective-permute-start | bytes 393224 | tf_op jit(solution)/shard_map/ppermute | solution.py:25
  5.5 6.1 %collective-permute-start = (bf16[64,1024]{1,0:T(8,128)(2,1)S(1)}, bf16[64,1024]{1,0:T(8,128)(2,1)S(1)}, u32[]{:S(2)}, u32[]{:S(2)}) collective-permute-start(bf16[64,1024]{1,0:T(8,128)(2,1)S(1)} %get-tuple-element.45), channel_id=1, source_target_pairs={{0,8},{8,0},{16,24},{24,16},{1,9},{9,1},{17,25},{25,17},{2,10},{10... | collective-permute-start | bytes 393224 | tf_op jit(solution)/shard_map/ppermute | solution.py:25
  11.4 1.0 copy-start.1
  11.4 1.0 copy-start.2
  16.5 8.7 %collective-permute-start.10 = (bf16[128,192]{1,0:T(8,128)(2,1)S(1)}, bf16[128,192]{1,0:T(8,128)(2,1)S(1)}, u32[]{:S(2)}, u32[]{:S(2)}) collective-permute-start(bf16[128,192]{1,0:T(8,128)(2,1)S(1)} %get-tuple-element.28), channel_id=1, source_target_pairs={{0,1},{1,0},{2,3},{3,2},{4,5},{5,4},{6,7},{7,6},{8,9},{9,8},{10,11... | collective-permute-start | bytes 147464 | tf_op jit(solution)/shard_map/ppermute | solution.py:25
  18.7 55.5 %collective-permute-start.3 = (bf16[16,7680]{1,0:T(8,128)(2,1)S(1)}, bf16[16,7680]{1,0:T(8,128)(2,1)S(1)}, u32[]{:S(2)}, u32[]{:S(2)}) collective-permute-start(bf16[16,7680]{1,0:T(8,128)(2,1)S(1)} %get-tuple-element.21), channel_id=1, source_target_pairs={{0,3},{1,2},{2,1},{3,0},{4,7},{5,6},{6,5},{7,4},{8,11},{9,10},{10,... | collective-permute-start | bytes 737288 | tf_op jit(solution)/shard_map/ppermute | solution.py:25
  20.2 54.0 %collective-permute-start.4 = (bf16[16,7680]{1,0:T(8,128)(2,1)S(1)}, bf16[16,7680]{1,0:T(8,128)(2,1)S(1)}, u32[]{:S(2)}, u32[]{:S(2)}) collective-permute-start(bf16[16,7680]{1,0:T(8,128)(2,1)S(1)} %get-tuple-element.22), channel_id=1, source_target_pairs={{0,2},{1,3},{2,0},{3,1},{4,6},{5,7},{6,4},{7,5},{8,10},{9,11},{10,... | collective-permute-start | bytes 737288 | tf_op jit(solution)/shard_map/ppermute | solution.py:25
  20.3 30.5 %collective-permute-start.6 = (bf16[16,7680]{1,0:T(8,128)(2,1)S(1)}, bf16[16,7680]{1,0:T(8,128)(2,1)S(1)}, u32[]{:S(2)}, u32[]{:S(2)}) collective-permute-start(bf16[16,7680]{1,0:T(8,128)(2,1)S(1)} %get-tuple-element.25), channel_id=1, source_target_pairs={{0,3},{1,2},{2,1},{3,0},{4,7},{5,6},{6,5},{7,4},{8,11},{9,10},{10,... | collective-permute-start | bytes 737288 | tf_op jit(solution)/shard_map/ppermute | solution.py:25
  23.2 29.2 %collective-permute-start.7 = (bf16[16,7680]{1,0:T(8,128)(2,1)S(1)}, bf16[16,7680]{1,0:T(8,128)(2,1)S(1)}, u32[]{:S(2)}, u32[]{:S(2)}) collective-permute-start(bf16[16,7680]{1,0:T(8,128)(2,1)S(1)} %get-tuple-element.26), channel_id=1, source_target_pairs={{0,2},{1,3},{2,0},{3,1},{4,6},{5,7},{6,4},{7,5},{8,10},{9,11},{10,... | collective-permute-start | bytes 737288 | tf_op jit(solution)/shard_map/ppermute | solution.py:25
  25.3 18.2 %collective-permute-start.11 = (bf16[128,192]{1,0:T(8,128)(2,1)S(1)}, bf16[128,192]{1,0:T(8,128)(2,1)S(1)}, u32[]{:S(2)}, u32[]{:S(2)}) collective-permute-start(bf16[128,192]{1,0:T(8,128)(2,1)S(1)} %add_convert_fusion.3), channel_id=1, source_target_pairs={{0,2},{1,3},{2,0},{3,1},{4,6},{5,7},{6,4},{7,5},{8,10},{9,11},{10,... | collective-permute-start | bytes 147464 | tf_op jit(solution)/shard_map/ppermute | solution.py:25
  43.4 5.2 %collective-permute-start.12 = (bf16[128,192]{1,0:T(8,128)(2,1)S(1)}, bf16[128,192]{1,0:T(8,128)(2,1)S(1)}, u32[]{:S(2)}, u32[]{:S(2)}) collective-permute-start(bf16[128,192]{1,0:T(8,128)(2,1)S(1)} %add_convert_fusion.2), channel_id=1, source_target_pairs={{0,4},{1,5},{2,6},{3,7},{4,0},{5,1},{6,2},{7,3},{8,12},{9,13},{10,... | collective-permute-start | bytes 147464 | tf_op jit(solution)/shard_map/ppermute | solution.py:25
  48.7 13.8 %collective-permute-start.8 = (bf16[16,7680]{1,0:T(8,128)(2,1)S(1)}, bf16[16,7680]{1,0:T(8,128)(2,1)S(1)}, u32[]{:S(2)}, u32[]{:S(2)}) collective-permute-start(bf16[16,7680]{1,0:T(8,128)(2,1)S(1)} %get-tuple-element.27), channel_id=1, source_target_pairs={{0,1},{1,0},{2,3},{3,2},{4,5},{5,4},{6,7},{7,6},{8,9},{9,8},{10,11... | collective-permute-start | bytes 737288 | tf_op jit(solution)/shard_map/ppermute | solution.py:25
  50.8 13.5 %collective-permute-start.13 = (bf16[32,3840]{1,0:T(8,128)(2,1)S(1)}, bf16[32,3840]{1,0:T(8,128)(2,1)S(1)}, u32[]{:S(2)}, u32[]{:S(2)}) collective-permute-start(bf16[32,3840]{1,0:T(8,128)(2,1)S(1)} %get-tuple-element.36), channel_id=1, source_target_pairs={{0,3},{1,2},{2,1},{3,0},{4,7},{5,6},{6,5},{7,4},{8,11},{9,10},{10,... | collective-permute-start | bytes 737288 | tf_op jit(solution)/shard_map/ppermute | solution.py:25
  52.4 15.3 %collective-permute-start.15 = (bf16[32,3840]{1,0:T(8,128)(2,1)S(1)}, bf16[32,3840]{1,0:T(8,128)(2,1)S(1)}, u32[]{:S(2)}, u32[]{:S(2)}) collective-permute-start(bf16[32,3840]{1,0:T(8,128)(2,1)S(1)} %get-tuple-element.37), channel_id=1, source_target_pairs={{0,1},{1,0},{2,3},{3,2},{4,5},{5,4},{6,7},{7,6},{8,9},{9,8},{10,11... | collective-permute-start | bytes 737288 | tf_op jit(solution)/shard_map/ppermute | solution.py:25
  62.5 9.1 %collective-permute-start.14 = (bf16[32,3840]{1,0:T(8,128)(2,1)S(1)}, bf16[32,3840]{1,0:T(8,128)(2,1)S(1)}, u32[]{:S(2)}, u32[]{:S(2)}) collective-permute-start(bf16[32,3840]{1,0:T(8,128)(2,1)S(1)} %get-tuple-element.38), channel_id=1, source_target_pairs={{0,2},{1,3},{2,0},{3,1},{4,6},{5,7},{6,4},{7,5},{8,10},{9,11},{10,... | collective-permute-start | bytes 737288 | tf_op jit(solution)/shard_map/ppermute | solution.py:25
  64.3 10.0 %collective-permute-start.5 = (bf16[16,7680]{1,0:T(8,128)(2,1)S(1)}, bf16[16,7680]{1,0:T(8,128)(2,1)S(1)}, u32[]{:S(2)}, u32[]{:S(2)}) collective-permute-start(bf16[16,7680]{1,0:T(8,128)(2,1)S(1)} %get-tuple-element.23), channel_id=1, source_target_pairs={{0,1},{1,0},{2,3},{3,2},{4,5},{5,4},{6,7},{7,6},{8,9},{9,8},{10,11... | collective-permute-start | bytes 737288 | tf_op jit(solution)/shard_map/ppermute | solution.py:25
  67.7 13.0 %collective-permute-start.9 = (bf16[16,7680]{1,0:T(8,128)(2,1)S(1)}, bf16[16,7680]{1,0:T(8,128)(2,1)S(1)}, u32[]{:S(2)}, u32[]{:S(2)}) collective-permute-start(bf16[16,7680]{1,0:T(8,128)(2,1)S(1)} %add_convert_fusion), channel_id=1, source_target_pairs={{0,4},{1,5},{2,6},{3,7},{4,0},{5,1},{6,2},{7,3},{8,12},{9,13},{10,... | collective-permute-start | bytes 737288 | tf_op jit(solution)/shard_map/ppermute | solution.py:25
  71.6 9.2 %copy-start.3 = (bf16[2,64,3840]{2,1,0:T(8,128)(2,1)S(1)}, bf16[2,64,3840]{2,1,0:T(8,128)(2,1)}, u32[]{:S(2)}) copy-start(bf16[2,64,3840]{2,1,0:T(8,128)(2,1)} %param.12) | copy-start | bytes 2949124
  71.7 10.3 %collective-permute-start.16 = (bf16[16,3840]{1,0:T(8,128)(2,1)S(1)}, bf16[16,3840]{1,0:T(8,128)(2,1)S(1)}, u32[]{:S(2)}, u32[]{:S(2)}) collective-permute-start(bf16[16,3840]{1,0:T(8,128)(2,1)S(1)} %slice.362), channel_id=1, source_target_pairs={{0,4},{1,5},{2,6},{3,7},{4,0},{5,1},{6,2},{7,3},{8,12},{9,13},{10,... | collective-permute-start | bytes 368648 | tf_op jit(solution)/shard_map/ppermute | solution.py:25
  82.2 38.1 %collective-permute-start.22 = (bf16[16,11520]{1,0:T(8,128)(2,1)S(1)}, bf16[16,11520]{1,0:T(8,128)(2,1)S(1)}, u32[]{:S(2)}, u32[]{:S(2)}) collective-permute-start(bf16[16,11520]{1,0:T(8,128)(2,1)S(1)} %pad_maximum_fusion), channel_id=1, source_target_pairs={{0,3},{1,2},{2,1},{3,0},{4,7},{5,6},{6,5},{7,4},{8,11},{9,10},{10,... | collective-permute-start | bytes 1105928 | tf_op jit(solution)/shard_map/ppermute | solution.py:25
  84.5 34.6 %collective-permute-start.20 = (bf16[16,11520]{1,0:T(8,128)(2,1)S(1)}, bf16[16,11520]{1,0:T(8,128)(2,1)S(1)}, u32[]{:S(2)}, u32[]{:S(2)}) collective-permute-start(bf16[16,11520]{1,0:T(8,128)(2,1)S(1)} %pad_maximum_fusion), channel_id=1, source_target_pairs={{0,2},{1,3},{2,0},{3,1},{4,6},{5,7},{6,4},{7,5},{8,10},{9,11},{10,... | collective-permute-start | bytes 1105928 | tf_op jit(solution)/shard_map/ppermute | solution.py:25
  85.6 11.2 %collective-permute-start.18 = (bf16[16,11520]{1,0:T(8,128)(2,1)S(1)}, bf16[16,11520]{1,0:T(8,128)(2,1)S(1)}, u32[]{:S(2)}, u32[]{:S(2)}) collective-permute-start(bf16[16,11520]{1,0:T(8,128)(2,1)S(1)} %pad_maximum_fusion), channel_id=1, source_target_pairs={{0,1},{1,0},{2,3},{3,2},{4,5},{5,4},{6,7},{7,6},{8,9},{9,8},{10,11... | collective-permute-start | bytes 1105928 | tf_op jit(solution)/shard_map/ppermute | solution.py:25
  85.7 21.8 %collective-permute-start.17 = (bf16[16,11520]{1,0:T(8,128)(2,1)S(1)}, bf16[16,11520]{1,0:T(8,128)(2,1)S(1)}, u32[]{:S(2)}, u32[]{:S(2)}) collective-permute-start(bf16[16,11520]{1,0:T(8,128)(2,1)S(1)} %pad_maximum_fusion), channel_id=1, source_target_pairs={{0,4},{1,5},{2,6},{3,7},{4,0},{5,1},{6,2},{7,3},{8,12},{9,13},{10,... | collective-permute-start | bytes 1105928 | tf_op jit(solution)/shard_map/ppermute | solution.py:25
  107.6 12.8 %collective-permute-start.23 = (bf16[16,3840]{1,0:T(8,128)(2,1)S(1)}, bf16[16,3840]{1,0:T(8,128)(2,1)S(1)}, u32[]{:S(2)}, u32[]{:S(2)}) collective-permute-start(bf16[16,3840]{1,0:T(8,128)(2,1)S(1)} %get-tuple-element.43), channel_id=1, source_target_pairs={{0,3},{1,2},{2,1},{3,0},{4,7},{5,6},{6,5},{7,4},{8,11},{9,10},{10,... | collective-permute-start | bytes 368648 | tf_op jit(solution)/shard_map/ppermute | solution.py:25
  111.7 7.5 %collective-permute-start.21 = (bf16[16,3840]{1,0:T(8,128)(2,1)S(1)}, bf16[16,3840]{1,0:T(8,128)(2,1)S(1)}, u32[]{:S(2)}, u32[]{:S(2)}) collective-permute-start(bf16[16,3840]{1,0:T(8,128)(2,1)S(1)} %get-tuple-element.43), channel_id=1, source_target_pairs={{0,2},{1,3},{2,0},{3,1},{4,6},{5,7},{6,4},{7,5},{8,10},{9,11},{10,... | collective-permute-start | bytes 368648 | tf_op jit(solution)/shard_map/ppermute | solution.py:25
  111.8 4.9 %collective-permute-start.19 = (bf16[16,3840]{1,0:T(8,128)(2,1)S(1)}, bf16[16,3840]{1,0:T(8,128)(2,1)S(1)}, u32[]{:S(2)}, u32[]{:S(2)}) collective-permute-start(bf16[16,3840]{1,0:T(8,128)(2,1)S(1)} %get-tuple-element.43), channel_id=1, source_target_pairs={{0,1},{1,0},{2,3},{3,2},{4,5},{5,4},{6,7},{7,6},{8,9},{9,8},{10,11... | collective-permute-start | bytes 368648 | tf_op jit(solution)/shard_map/ppermute | solution.py:25
  112.5 17.9 %slice-start = ((s8[15728640]{0:T(1024)(128)(4,1)}), s8[4194304]{0:T(1024)(128)(4,1)S(1)}, s32[]{:S(2)}) async-start(s8[15728640]{0:T(1024)(128)(4,1)} %bitcast.53), calls=%async_computation | async-start | bytes 8388608
  116.6 12.8 %collective-permute-start.30 = (bf16[16,7680]{1,0:T(8,128)(2,1)S(1)}, bf16[16,7680]{1,0:T(8,128)(2,1)S(1)}, u32[]{:S(2)}, u32[]{:S(2)}) collective-permute-start(bf16[16,7680]{1,0:T(8,128)(2,1)S(1)} %get-tuple-element.41), channel_id=1, source_target_pairs={{0,3},{1,2},{2,1},{3,0},{4,7},{5,6},{6,5},{7,4},{8,11},{9,10},{10,... | collective-permute-start | bytes 737288 | tf_op jit(solution)/shard_map/ppermute | solution.py:25
  119.1 10.2 %collective-permute-start.29 = (bf16[16,7680]{1,0:T(8,128)(2,1)S(1)}, bf16[16,7680]{1,0:T(8,128)(2,1)S(1)}, u32[]{:S(2)}, u32[]{:S(2)}) collective-permute-start(bf16[16,7680]{1,0:T(8,128)(2,1)S(1)} %get-tuple-element.41), channel_id=1, source_target_pairs={{0,2},{1,3},{2,0},{3,1},{4,6},{5,7},{6,4},{7,5},{8,10},{9,11},{10,... | collective-permute-start | bytes 737288 | tf_op jit(solution)/shard_map/ppermute | solution.py:25
  119.2 10.1 %collective-permute-start.28 = (bf16[16,7680]{1,0:T(8,128)(2,1)S(1)}, bf16[16,7680]{1,0:T(8,128)(2,1)S(1)}, u32[]{:S(2)}, u32[]{:S(2)}) collective-permute-start(bf16[16,7680]{1,0:T(8,128)(2,1)S(1)} %get-tuple-element.41), channel_id=1, source_target_pairs={{0,1},{1,0},{2,3},{3,2},{4,5},{5,4},{6,7},{7,6},{8,9},{9,8},{10,11... | collective-permute-start | bytes 737288 | tf_op jit(solution)/shard_map/ppermute | solution.py:25
  120.4 9.9 %slice-start.1 = ((s8[15728640]{0:T(1024)(128)(4,1)}), s8[4194304]{0:T(1024)(128)(4,1)S(1)}, s32[]{:S(2)}) async-start(s8[15728640]{0:T(1024)(128)(4,1)} %bitcast.53), calls=%async_computation.1 | async-start | bytes 8388608
  120.4 9.9 %slice-start.2 = ((s8[15728640]{0:T(1024)(128)(4,1)}), s8[4194304]{0:T(1024)(128)(4,1)S(1)}, s32[]{:S(2)}) async-start(s8[15728640]{0:T(1024)(128)(4,1)} %bitcast.53), calls=%async_computation.2 | async-start | bytes 8388608
  122.1 1.3 collective-permute-start.26
  123.4 7.0 %slice-start.3 = ((s8[15728640]{0:T(1024)(128)(4,1)}), s8[3145728]{0:T(1024)(128)(4,1)S(1)}, s32[]{:S(2)}) async-start(s8[15728640]{0:T(1024)(128)(4,1)} %bitcast.53), calls=%async_computation.3 | async-start | bytes 6291456
  123.4 3.8 %collective-permute-start.27 = (bf16[128,64]{0,1:T(8,128)(2,1)S(1)}, bf16[128,64]{0,1:T(8,128)(2,1)S(1)}, u32[]{:S(2)}, u32[]{:S(2)}) collective-permute-start(bf16[128,64]{0,1:T(8,128)(2,1)S(1)} %add_convert_fusion.7), channel_id=1, source_target_pairs={{0,16},{8,24},{16,0},{24,8},{1,17},{9,25},{17,1},{25,9},{2,18},{10... | collective-permute-start | bytes 49160 | tf_op jit(solution)/shard_map/ppermute | solution.py:25
  125.5 15.1 %collective-permute-start.24 = (bf16[64,1024]{1,0:T(8,128)(2,1)S(1)}, bf16[64,1024]{1,0:T(8,128)(2,1)S(1)}, u32[]{:S(2)}, u32[]{:S(2)}) collective-permute-start(bf16[64,1024]{1,0:T(8,128)(2,1)S(1)} %slice.361), channel_id=1, source_target_pairs={{0,8},{8,0},{16,24},{24,16},{1,9},{9,1},{17,25},{25,17},{2,10},{10... | collective-permute-start | bytes 393224 | tf_op jit(solution)/shard_map/ppermute | solution.py:25
  133.7 5.2 %collective-permute-start.33 = (bf16[128,128]{0,1:T(8,128)(2,1)S(1)}, bf16[128,128]{0,1:T(8,128)(2,1)S(1)}, u32[]{:S(2)}, u32[]{:S(2)}) collective-permute-start(bf16[128,128]{0,1:T(8,128)(2,1)S(1)} %pad_maximum_fusion.1), channel_id=1, source_target_pairs={{0,8},{8,0},{16,24},{24,16},{1,9},{9,1},{17,25},{25,17},{2,10},{10... | collective-permute-start | bytes 98312 | tf_op jit(solution)/shard_map/ppermute | solution.py:25
  136.9 7.7 %collective-permute-start.31 = (bf16[64,1024]{1,0:T(8,128)(2,1)S(1)}, bf16[64,1024]{1,0:T(8,128)(2,1)S(1)}, u32[]{:S(2)}, u32[]{:S(2)}) collective-permute-start(bf16[64,1024]{1,0:T(8,128)(2,1)S(1)} %slice.360), channel_id=1, source_target_pairs={{0,8},{8,0},{16,24},{24,16},{1,9},{9,1},{17,25},{25,17},{2,10},{10... | collective-permute-start | bytes 393224 | tf_op jit(solution)/shard_map/ppermute | solution.py:25
  138.9 4.0 %collective-permute-start.34 = (bf16[128,128]{0,1:T(8,128)(2,1)S(1)}, bf16[128,128]{0,1:T(8,128)(2,1)S(1)}, u32[]{:S(2)}, u32[]{:S(2)}) collective-permute-start(bf16[128,128]{0,1:T(8,128)(2,1)S(1)} %add_convert_fusion.6), channel_id=1, source_target_pairs={{0,16},{8,24},{16,0},{24,8},{1,17},{9,25},{17,1},{25,9},{2,18},{10... | collective-permute-start | bytes 98312 | tf_op jit(solution)/shard_map/ppermute | solution.py:25
  140.6 5.8 %collective-permute-start.25 = (bf16[32,1024]{1,0:T(8,128)(2,1)S(1)}, bf16[32,1024]{1,0:T(8,128)(2,1)S(1)}, u32[]{:S(2)}, u32[]{:S(2)}) collective-permute-start(bf16[32,1024]{1,0:T(8,128)(2,1)S(1)} %slice.364), channel_id=1, source_target_pairs={{0,16},{8,24},{16,0},{24,8},{1,17},{9,25},{17,1},{25,9},{2,18},{10... | collective-permute-start | bytes 196616 | tf_op jit(solution)/shard_map/ppermute | solution.py:25
  144.7 4.3 %collective-permute-start.32 = (bf16[32,1024]{1,0:T(8,128)(2,1)S(1)}, bf16[32,1024]{1,0:T(8,128)(2,1)S(1)}, u32[]{:S(2)}, u32[]{:S(2)}) collective-permute-start(bf16[32,1024]{1,0:T(8,128)(2,1)S(1)} %slice.363), channel_id=1, source_target_pairs={{0,16},{8,24},{16,0},{24,8},{1,17},{9,25},{17,1},{25,9},{2,18},{10... | collective-permute-start | bytes 196616 | tf_op jit(solution)/shard_map/ppermute | solution.py:25
where the time goes:
time: 150 us
  waiting for transfers between devices  67.1 us (45%)
  starting transfers between devices  47.6 us (32%)
  matrix products  16.7 us (11%)
  Pallas kernels  9.94 us (7%)
  other arithmetic  4.53 us (3%)
  local copies, waits for them, and re-layouts  2.49 us (2%)
    ppermute x35, waiting for transfers between devices, exchange(): return lax.ppermute(value, axis, [(i, i ^ mask) for i in range(size)])  67.1 us
    ppermute x35, starting transfers between devices, exchange(): return lax.ppermute(value, axis, [(i, i ^ mask) for i in range(size)])  47.6 us
    dot_general x25, matrix products, dot(): lax.dot_general(left, right, (dims, ((), ())), preferred_element_type=sin...  16.7 us
    pallas_call x1, Pallas kernels, load(): pl.pallas_call(kernel, in_specs=[anywhere] * 2, out_specs=[anywhere] * 2,...  5.83 us
    pallas_call x1, Pallas kernels, project(): pl.pallas_call(kernel, in_specs=[vmem] * 4 + [pl.BlockSpec(memory_space=p...  4.11 us
  transfers between devices with their start and end apart: 35, of which 16 were waited for; matrix products, arithmetic and copies ran while one was open for 14% of the time, Pallas kernels for 4%

commit v1 on v0

--- a/solution.py
+++ b/solution.py
@@ -310,9 +310,8 @@
         low_down, cot.astype(single), ((0,), (0,)), HIGHEST
     )
 
-    gate_up_output_factor_gradient = gradient_scale * jnp.stack(
-        [dot(low_all[k], back_all[k], ((0,), (0,))) for k in range(2)]
-    )
+    factor_parts = jnp.stack([dot(low_all[k], back_all[k], ((0,), (0,))) for k in range(2)])
+    gate_up_output_factor_gradient = gradient_scale * factor_parts
     back_low = sum_all(
         jnp.concatenate(
             [dot(back_all[k], gate_up_output_factor[k], ((1,), (1,))) for k in range(2)], axis=1

time: 150 us -> 150 us (level)
  no operation moved by 1% of the time
where the time goes in v1:
time: 150 us
  waiting for transfers between devices  67.1 us (45%)
  starting transfers between devices  47.6 us (32%)
  matrix products  16.7 us (11%)
  Pallas kernels  9.94 us (7%)
  other arithmetic  4.53 us (3%)
  local copies, waits for them, and re-layouts  2.49 us (2%)
    ppermute x35, waiting for transfers between devices, exchange(): return lax.ppermute(value, axis, [(i, i ^ mask) for i in range(size)])  67.1 us
    ppermute x35, starting transfers between devices, exchange(): return lax.ppermute(value, axis, [(i, i ^ mask) for i in range(size)])  47.6 us
    dot_general x25, matrix products, dot(): lax.dot_general(left, right, (dims, ((), ())), preferred_element_type=sin...  16.7 us
    pallas_call x1, Pallas kernels, load(): pl.pallas_call(kernel, in_specs=[anywhere] * 2, out_specs=[anywhere] * 2,...  5.83 us
    pallas_call x1, Pallas kernels, project(): pl.pallas_call(kernel, in_specs=[vmem] * 4 + [pl.BlockSpec(memory_space=p...  4.11 us
  transfers between devices with their start and end apart: 35, of which 16 were waited for; matrix products, arithmetic and copies ran while one was open for 14% of the time, Pallas kernels for 4%

profile of v1, /device:TPU:0, one launch (start us, length us, event | category | flops | bytes accessed | tf_op | source)
XLA Modules:
  0.0 149.7 jit_solution(4428409735466348009)
XLA Ops:
  0.6 0.9 constant_dynamic-update-slice_fusion.1
  1.6 0.9 constant_dynamic-update-slice_fusion
  2.4 2.5 %collective-permute-start.2 = (bf16[64,1024]{1,0:T(8,128)(2,1)S(1)}, bf16[64,1024]{1,0:T(8,128)(2,1)S(1)}, u32[]{:S(2)}, u32[]{:S(2)}) collective-permute-start(bf16[64,1024]{1,0:T(8,128)(2,1)S(1)} %get-tuple-element.45), channel_id=1, source_target_pairs={{0,24},{8,16},{16,8},{24,0},{1,25},{9,17},{17,9},{25,1},{2,26},{10... | collective-permute-start | bytes 393224 | tf_op jit(solution)/shard_map/ppermute | solution.py:25
  5.6 5.8 %shard_map.127 = (bf16[3840,1024]{1,0:T(8,128)(2,1)S(1)}, bf16[1024,3840]{1,0:T(8,128)(2,1)S(1)}) custom-call(bf16[3840,1024]{1,0:T(8,128)(2,1)} %down_ref.1, bf16[2,1024,3840]{2,1,0:T(8,128)(2,1)} %refs_4_.1), custom_call_target="tpu_custom_call" | custom-call | flops 10000000000 | bytes 31457280 | tf_op jit(solution)/shard_map/pallas_call | solution.py:75
  12.4 4.1 %shard_map.128 = (bf16[16,7680]{1,0:T(8,128)(2,1)S(1)}, bf16[16,7680]{1,0:T(8,128)(2,1)S(1)}, bf16[16,7680]{1,0:T(8,128)(2,1)S(1)}, bf16[16,7680]{1,0:T(8,128)(2...) custom-call(bf16[128,1024]{1,0:T(8,128)(2,1)S(1)} %get-tuple-element, ...), custom_call_target="tpu_custom_call" | custom-call | flops 8053063680 | bytes 15728640 | tf_op jit(solution)/shard_map/pallas_call | solution.py:135
  16.5 2.2 %collective-permute-start.10 = (bf16[128,192]{1,0:T(8,128)(2,1)S(1)}, bf16[128,192]{1,0:T(8,128)(2,1)S(1)}, u32[]{:S(2)}, u32[]{:S(2)}) collective-permute-start(bf16[128,192]{1,0:T(8,128)(2,1)S(1)} %get-tuple-element.28), channel_id=1, source_target_pairs={{0,1},{1,0},{2,3},{3,2},{4,5},{5,4},{6,7},{7,6},{8,9},{9,8},{10,11... | collective-permute-start | bytes 147464 | tf_op jit(solution)/shard_map/ppermute | solution.py:25
  18.7 1.5 %collective-permute-start.3 = (bf16[16,7680]{1,0:T(8,128)(2,1)S(1)}, bf16[16,7680]{1,0:T(8,128)(2,1)S(1)}, u32[]{:S(2)}, u32[]{:S(2)}) collective-permute-start(bf16[16,7680]{1,0:T(8,128)(2,1)S(1)} %get-tuple-element.21), channel_id=1, source_target_pairs={{0,3},{1,2},{2,1},{3,0},{4,7},{5,6},{6,5},{7,4},{8,11},{9,10},{10,... | collective-permute-start | bytes 737288 | tf_op jit(solution)/shard_map/ppermute | solution.py:25
  20.3 2.9 %collective-permute-start.6 = (bf16[16,7680]{1,0:T(8,128)(2,1)S(1)}, bf16[16,7680]{1,0:T(8,128)(2,1)S(1)}, u32[]{:S(2)}, u32[]{:S(2)}) collective-permute-start(bf16[16,7680]{1,0:T(8,128)(2,1)S(1)} %get-tuple-element.25), channel_id=1, source_target_pairs={{0,3},{1,2},{2,1},{3,0},{4,7},{5,6},{6,5},{7,4},{8,11},{9,10},{10,... | collective-permute-start | bytes 737288 | tf_op jit(solution)/shard_map/ppermute | solution.py:25
  23.6 1.6 %collective-permute-done.10 = bf16[128,192]{1,0:T(8,128)(2,1)S(1)} collective-permute-done((bf16[128,192]{1,0:T(8,128)(2,1)S(1)}, bf16[128,192]{1,0:T(8,128)(2,1)S(1)}, u32[]{:S(2)}, u32[]{:S(2)}) %collective-permute-start.10) | collective-permute-done | bytes 49184 | tf_op jit(solution)/shard_map/ppermute | solution.py:25
  25.3 1.3 collective-permute-start.11
  26.6 2.7 %fusion.84 = (bf16[128,3840]{1,0:T(8,128)(2,1)S(1)}, f32[128,3840]{1,0:T(8,128)S(1)}) fusion(bf16[3840,1024]{1,0:T(8,128)(2,1)S(1)} %get-tuple-element.29, bf16[256,1024]{1,0:T(8,128)(2,1)S(1)} %convolution_convert_fusion), kind=kOutput, calls=%fused_computation.181 | convolution fusion | flops 1007124480 | bytes 11075584 | tf_op jit(solution)/shard_map/dot_general | solution.py:18
  29.3 14.1 %collective-permute-done.11 = bf16[128,192]{1,0:T(8,128)(2,1)S(1)} collective-permute-done((bf16[128,192]{1,0:T(8,128)(2,1)S(1)}, bf16[128,192]{1,0:T(8,128)(2,1)S(1)}, u32[]{:S(2)}, u32[]{:S(2)}) %collective-permute-start.11) | collective-permute-done | bytes 49184 | tf_op jit(solution)/shard_map/ppermute | solution.py:25
  43.4 2.8 %collective-permute-start.12 = (bf16[128,192]{1,0:T(8,128)(2,1)S(1)}, bf16[128,192]{1,0:T(8,128)(2,1)S(1)}, u32[]{:S(2)}, u32[]{:S(2)}) collective-permute-start(bf16[128,192]{1,0:T(8,128)(2,1)S(1)} %add_convert_fusion.2), channel_id=1, source_target_pairs={{0,4},{1,5},{2,6},{3,7},{4,0},{5,1},{6,2},{7,3},{8,12},{9,13},{10,... | collective-permute-start | bytes 147464 | tf_op jit(solution)/shard_map/ppermute | solution.py:25
  46.3 2.4 %collective-permute-done.12 = bf16[128,192]{1,0:T(8,128)(2,1)S(1)} collective-permute-done((bf16[128,192]{1,0:T(8,128)(2,1)S(1)}, bf16[128,192]{1,0:T(8,128)(2,1)S(1)}, u32[]{:S(2)}, u32[]{:S(2)}) %collective-permute-start.12) | collective-permute-done | bytes 49184 | tf_op jit(solution)/shard_map/ppermute | solution.py:25
  48.7 1.6 %collective-permute-start.8 = (bf16[16,7680]{1,0:T(8,128)(2,1)S(1)}, bf16[16,7680]{1,0:T(8,128)(2,1)S(1)}, u32[]{:S(2)}, u32[]{:S(2)}) collective-permute-start(bf16[16,7680]{1,0:T(8,128)(2,1)S(1)} %get-tuple-element.27), channel_id=1, source_target_pairs={{0,1},{1,0},{2,3},{3,2},{4,5},{5,4},{6,7},{7,6},{8,9},{9,8},{10,11... | collective-permute-start | bytes 737288 | tf_op jit(solution)/shard_map/ppermute | solution.py:25
  50.8 1.6 %collective-permute-start.13 = (bf16[32,3840]{1,0:T(8,128)(2,1)S(1)}, bf16[32,3840]{1,0:T(8,128)(2,1)S(1)}, u32[]{:S(2)}, u32[]{:S(2)}) collective-permute-start(bf16[32,3840]{1,0:T(8,128)(2,1)S(1)} %get-tuple-element.36), channel_id=1, source_target_pairs={{0,3},{1,2},{2,1},{3,0},{4,7},{5,6},{6,5},{7,4},{8,11},{9,10},{10,... | collective-permute-start | bytes 737288 | tf_op jit(solution)/shard_map/ppermute | solution.py:25
  52.4 1.5 collective-permute-start.15
  53.9 8.6 %collective-permute-done.8 = bf16[16,7680]{1,0:T(8,128)(2,1)S(1)} collective-permute-done((bf16[16,7680]{1,0:T(8,128)(2,1)S(1)}, bf16[16,7680]{1,0:T(8,128)(2,1)S(1)}, u32[]{:S(2)}, u32[]{:S(2)}) %collective-permute-start.8) | collective-permute-done | bytes 245792 | tf_op jit(solution)/shard_map/ppermute | solution.py:25
  62.5 1.7 %collective-permute-start.14 = (bf16[32,3840]{1,0:T(8,128)(2,1)S(1)}, bf16[32,3840]{1,0:T(8,128)(2,1)S(1)}, u32[]{:S(2)}, u32[]{:S(2)}) collective-permute-start(bf16[32,3840]{1,0:T(8,128)(2,1)S(1)} %get-tuple-element.38), channel_id=1, source_target_pairs={{0,2},{1,3},{2,0},{3,1},{4,6},{5,7},{6,4},{7,5},{8,10},{9,11},{10,... | collective-permute-start | bytes 737288 | tf_op jit(solution)/shard_map/ppermute | solution.py:25
  64.9 2.8 %collective-permute-done.15 = bf16[32,3840]{1,0:T(8,128)(2,1)S(1)} collective-permute-done((bf16[32,3840]{1,0:T(8,128)(2,1)S(1)}, bf16[32,3840]{1,0:T(8,128)(2,1)S(1)}, u32[]{:S(2)}, u32[]{:S(2)}) %collective-permute-start.15) | collective-permute-done | bytes 245792 | tf_op jit(solution)/shard_map/ppermute | solution.py:25
  67.7 2.5 %collective-permute-start.9 = (bf16[16,7680]{1,0:T(8,128)(2,1)S(1)}, bf16[16,7680]{1,0:T(8,128)(2,1)S(1)}, u32[]{:S(2)}, u32[]{:S(2)}) collective-permute-start(bf16[16,7680]{1,0:T(8,128)(2,1)S(1)} %add_convert_fusion), channel_id=1, source_target_pairs={{0,4},{1,5},{2,6},{3,7},{4,0},{5,1},{6,2},{7,3},{8,12},{9,13},{10,... | collective-permute-start | bytes 737288 | tf_op jit(solution)/shard_map/ppermute | solution.py:25
  70.2 1.4 collective-permute-done.14
  71.7 2.5 %collective-permute-start.16 = (bf16[16,3840]{1,0:T(8,128)(2,1)S(1)}, bf16[16,3840]{1,0:T(8,128)(2,1)S(1)}, u32[]{:S(2)}, u32[]{:S(2)}) collective-permute-start(bf16[16,3840]{1,0:T(8,128)(2,1)S(1)} %slice.362), channel_id=1, source_target_pairs={{0,4},{1,5},{2,6},{3,7},{4,0},{5,1},{6,2},{7,3},{8,12},{9,13},{10,... | collective-permute-start | bytes 368648 | tf_op jit(solution)/shard_map/ppermute | solution.py:25
  74.2 6.4 %collective-permute-done.9 = bf16[16,7680]{1,0:T(8,128)(2,1)S(1)} collective-permute-done((bf16[16,7680]{1,0:T(8,128)(2,1)S(1)}, bf16[16,7680]{1,0:T(8,128)(2,1)S(1)}, u32[]{:S(2)}, u32[]{:S(2)}) %collective-permute-start.9) | collective-permute-done | bytes 245792 | tf_op jit(solution)/shard_map/ppermute | solution.py:25
  81.3 0.7 collective-permute-done.16
  82.2 2.3 %collective-permute-start.22 = (bf16[16,11520]{1,0:T(8,128)(2,1)S(1)}, bf16[16,11520]{1,0:T(8,128)(2,1)S(1)}, u32[]{:S(2)}, u32[]{:S(2)}) collective-permute-start(bf16[16,11520]{1,0:T(8,128)(2,1)S(1)} %pad_maximum_fusion), channel_id=1, source_target_pairs={{0,3},{1,2},{2,1},{3,0},{4,7},{5,6},{6,5},{7,4},{8,11},{9,10},{10,... | collective-permute-start | bytes 1105928 | tf_op jit(solution)/shard_map/ppermute | solution.py:25
  84.5 1.1 collective-permute-start.20
  85.7 2.8 %collective-permute-start.17 = (bf16[16,11520]{1,0:T(8,128)(2,1)S(1)}, bf16[16,11520]{1,0:T(8,128)(2,1)S(1)}, u32[]{:S(2)}, u32[]{:S(2)}) collective-permute-start(bf16[16,11520]{1,0:T(8,128)(2,1)S(1)} %pad_maximum_fusion), channel_id=1, source_target_pairs={{0,4},{1,5},{2,6},{3,7},{4,0},{5,1},{6,2},{7,3},{8,12},{9,13},{10,... | collective-permute-start | bytes 1105928 | tf_op jit(solution)/shard_map/ppermute | solution.py:25
  88.6 8.2 %collective-permute-done.18 = bf16[16,11520]{1,0:T(8,128)(2,1)S(1)} collective-permute-done((bf16[16,11520]{1,0:T(8,128)(2,1)S(1)}, bf16[16,11520]{1,0:T(8,128)(2,1)S(1)}, u32[]{:S(2)}, u32[]{:S(2)}) %collective-permute-start.18) | collective-permute-done | bytes 368672 | tf_op jit(solution)/shard_map/ppermute | solution.py:25
  96.8 10.8 %collective-permute-done.17 = bf16[16,11520]{1,0:T(8,128)(2,1)S(1)} collective-permute-done((bf16[16,11520]{1,0:T(8,128)(2,1)S(1)}, bf16[16,11520]{1,0:T(8,128)(2,1)S(1)}, u32[]{:S(2)}, u32[]{:S(2)}) %collective-permute-start.17) | collective-permute-done | bytes 368672 | tf_op jit(solution)/shard_map/ppermute | solution.py:25
  107.6 4.2 %collective-permute-start.23 = (bf16[16,3840]{1,0:T(8,128)(2,1)S(1)}, bf16[16,3840]{1,0:T(8,128)(2,1)S(1)}, u32[]{:S(2)}, u32[]{:S(2)}) collective-permute-start(bf16[16,3840]{1,0:T(8,128)(2,1)S(1)} %get-tuple-element.43), channel_id=1, source_target_pairs={{0,3},{1,2},{2,1},{3,0},{4,7},{5,6},{6,5},{7,4},{8,11},{9,10},{10,... | collective-permute-start | bytes 368648 | tf_op jit(solution)/shard_map/ppermute | solution.py:25
  112.5 4.1 %collective-permute-done.19 = bf16[16,3840]{1,0:T(8,128)(2,1)S(1)} collective-permute-done((bf16[16,3840]{1,0:T(8,128)(2,1)S(1)}, bf16[16,3840]{1,0:T(8,128)(2,1)S(1)}, u32[]{:S(2)}, u32[]{:S(2)}) %collective-permute-start.19) | collective-permute-done | bytes 122912 | tf_op jit(solution)/shard_map/ppermute | solution.py:25
  116.6 2.5 %collective-permute-start.30 = (bf16[16,7680]{1,0:T(8,128)(2,1)S(1)}, bf16[16,7680]{1,0:T(8,128)(2,1)S(1)}, u32[]{:S(2)}, u32[]{:S(2)}) collective-permute-start(bf16[16,7680]{1,0:T(8,128)(2,1)S(1)} %get-tuple-element.41), channel_id=1, source_target_pairs={{0,3},{1,2},{2,1},{3,0},{4,7},{5,6},{6,5},{7,4},{8,11},{9,10},{10,... | collective-permute-start | bytes 737288 | tf_op jit(solution)/shard_map/ppermute | solution.py:25
  119.2 1.1 collective-permute-start.28
  120.4 1.2 fusion.85
  122.1 1.2 convolution_multiply_fusion
  123.4 1.6 %collective-permute-start.27 = (bf16[128,64]{0,1:T(8,128)(2,1)S(1)}, bf16[128,64]{0,1:T(8,128)(2,1)S(1)}, u32[]{:S(2)}, u32[]{:S(2)}) collective-permute-start(bf16[128,64]{0,1:T(8,128)(2,1)S(1)} %add_convert_fusion.7), channel_id=1, source_target_pairs={{0,16},{8,24},{16,0},{24,8},{1,17},{9,25},{17,1},{25,9},{2,18},{10... | collective-permute-start | bytes 49160 | tf_op jit(solution)/shard_map/ppermute | solution.py:25
  125.7 1.5 collective-permute-done.27
  127.6 1.0 convolution_multiply_fusion.4
  128.6 0.7 collective-permute-done.28
  130.4 2.8 %fusion = f32[128,1024]{1,0:T(8,128)S(1)} fusion(bf16[2,1024,3840]{2,1,0:T(8,128)(2,1)S(1)} %bitcast.54, bf16[128,7680]{1,0:T(8,128)(2,1)S(1)} %constant_dynamic-update-slice_fusion.12), kind=kOutput, calls=%fused_computation | convolution fusion | flops 1006632960 | bytes 9371648 | tf_op jit(solution)/shard_map/dot_general | solution.py:18
  133.8 2.6 %fusion.6 = f32[128,1024]{1,0:T(8,128)S(1)} fusion(f32[128,1024]{1,0:T(8,128)S(1)} %fusion, bf16[2,1024,3840]{2,1,0:T(8,128)(2,1)S(1)} %bitcast.54, bf16[128,7680]{1,0:T(8,128)(2,1)S(1)} %constant_dynamic-update-slice_fusion.12), kind=kOutput, calls=%fused_computation.14 | convolution fusion | flops 1006764032 | bytes 9895936 | tf_op jit(solution)/shard_map/dot_general | solution.py:18
  137.4 1.4 maximum_multiply_fusion
  138.9 1.6 %collective-permute-start.34 = (bf16[128,128]{0,1:T(8,128)(2,1)S(1)}, bf16[128,128]{0,1:T(8,128)(2,1)S(1)}, u32[]{:S(2)}, u32[]{:S(2)}) collective-permute-start(bf16[128,128]{0,1:T(8,128)(2,1)S(1)} %add_convert_fusion.6), channel_id=1, source_target_pairs={{0,16},{8,24},{16,0},{24,8},{1,17},{9,25},{17,1},{25,9},{2,18},{10... | collective-permute-start | bytes 98312 | tf_op jit(solution)/shard_map/ppermute | solution.py:25
  141.1 1.8 %collective-permute-done.34 = bf16[128,128]{0,1:T(8,128)(2,1)S(1)} collective-permute-done((bf16[128,128]{0,1:T(8,128)(2,1)S(1)}, bf16[128,128]{0,1:T(8,128)(2,1)S(1)}, u32[]{:S(2)}, u32[]{:S(2)}) %collective-permute-start.34) | collective-permute-done | bytes 32800 | tf_op jit(solution)/shard_map/ppermute | solution.py:25
  143.8 0.8 maximum_multiply_fusion.1
  144.7 1.7 %collective-permute-start.32 = (bf16[32,1024]{1,0:T(8,128)(2,1)S(1)}, bf16[32,1024]{1,0:T(8,128)(2,1)S(1)}, u32[]{:S(2)}, u32[]{:S(2)}) collective-permute-start(bf16[32,1024]{1,0:T(8,128)(2,1)S(1)} %slice.363), channel_id=1, source_target_pairs={{0,16},{8,24},{16,0},{24,8},{1,17},{9,25},{17,1},{25,9},{2,18},{10... | collective-permute-start | bytes 196616 | tf_op jit(solution)/shard_map/ppermute | solution.py:25
  147.0 2.0 %collective-permute-done.32 = bf16[32,1024]{1,0:T(8,128)(2,1)S(1)} collective-permute-done((bf16[32,1024]{1,0:T(8,128)(2,1)S(1)}, bf16[32,1024]{1,0:T(8,128)(2,1)S(1)}, u32[]{:S(2)}, u32[]{:S(2)}) %collective-permute-start.32) | collective-permute-done | bytes 65568 | tf_op jit(solution)/shard_map/ppermute | solution.py:25
  (115 shorter events, 12.5 us)
Async XLA Ops:
  0.6 49.9 %copy-start = (bf16[3840,64]{0,1:T(8,128)(2,1)S(1)}, bf16[3840,64]{0,1:T(8,128)(2,1)}, u32[]{:S(2)}) copy-start(bf16[3840,64]{0,1:T(8,128)(2,1)} %param.13) | copy-start | bytes 1474564
  2.4 9.4 %collective-permute-start.2 = (bf16[64,1024]{1,0:T(8,128)(2,1)S(1)}, bf16[64,1024]{1,0:T(8,128)(2,1)S(1)}, u32[]{:S(2)}, u32[]{:S(2)}) collective-permute-start(bf16[64,1024]{1,0:T(8,128)(2,1)S(1)} %get-tuple-element.45), channel_id=1, source_target_pairs={{0,24},{8,16},{16,8},{24,0},{1,25},{9,17},{17,9},{25,1},{2,26},{10... | collective-permute-start | bytes 393224 | tf_op jit(solution)/shard_map/ppermute | solution.py:25
  4.9 6.9 %collective-permute-start.1 = (bf16[64,1024]{1,0:T(8,128)(2,1)S(1)}, bf16[64,1024]{1,0:T(8,128)(2,1)S(1)}, u32[]{:S(2)}, u32[]{:S(2)}) collective-permute-start(bf16[64,1024]{1,0:T(8,128)(2,1)S(1)} %get-tuple-element.45), channel_id=1, source_target_pairs={{0,16},{8,24},{16,0},{24,8},{1,17},{9,25},{17,1},{25,9},{2,18},{10... | collective-permute-start | bytes 393224 | tf_op jit(solution)/shard_map/ppermute | solution.py:25
  5.5 6.1 %collective-permute-start = (bf16[64,1024]{1,0:T(8,128)(2,1)S(1)}, bf16[64,1024]{1,0:T(8,128)(2,1)S(1)}, u32[]{:S(2)}, u32[]{:S(2)}) collective-permute-start(bf16[64,1024]{1,0:T(8,128)(2,1)S(1)} %get-tuple-element.45), channel_id=1, source_target_pairs={{0,8},{8,0},{16,24},{24,16},{1,9},{9,1},{17,25},{25,17},{2,10},{10... | collective-permute-start | bytes 393224 | tf_op jit(solution)/shard_map/ppermute | solution.py:25
  11.4 1.0 copy-start.1
  11.4 1.0 copy-start.2
  16.5 8.7 %collective-permute-start.10 = (bf16[128,192]{1,0:T(8,128)(2,1)S(1)}, bf16[128,192]{1,0:T(8,128)(2,1)S(1)}, u32[]{:S(2)}, u32[]{:S(2)}) collective-permute-start(bf16[128,192]{1,0:T(8,128)(2,1)S(1)} %get-tuple-element.28), channel_id=1, source_target_pairs={{0,1},{1,0},{2,3},{3,2},{4,5},{5,4},{6,7},{7,6},{8,9},{9,8},{10,11... | collective-permute-start | bytes 147464 | tf_op jit(solution)/shard_map/ppermute | solution.py:25
  18.7 55.5 %collective-permute-start.3 = (bf16[16,7680]{1,0:T(8,128)(2,1)S(1)}, bf16[16,7680]{1,0:T(8,128)(2,1)S(1)}, u32[]{:S(2)}, u32[]{:S(2)}) collective-permute-start(bf16[16,7680]{1,0:T(8,128)(2,1)S(1)} %get-tuple-element.21), channel_id=1, source_target_pairs={{0,3},{1,2},{2,1},{3,0},{4,7},{5,6},{6,5},{7,4},{8,11},{9,10},{10,... | collective-permute-start | bytes 737288 | tf_op jit(solution)/shard_map/ppermute | solution.py:25
  20.2 54.0 %collective-permute-start.4 = (bf16[16,7680]{1,0:T(8,128)(2,1)S(1)}, bf16[16,7680]{1,0:T(8,128)(2,1)S(1)}, u32[]{:S(2)}, u32[]{:S(2)}) collective-permute-start(bf16[16,7680]{1,0:T(8,128)(2,1)S(1)} %get-tuple-element.22), channel_id=1, source_target_pairs={{0,2},{1,3},{2,0},{3,1},{4,6},{5,7},{6,4},{7,5},{8,10},{9,11},{10,... | collective-permute-start | bytes 737288 | tf_op jit(solution)/shard_map/ppermute | solution.py:25
  20.3 30.5 %collective-permute-start.6 = (bf16[16,7680]{1,0:T(8,128)(2,1)S(1)}, bf16[16,7680]{1,0:T(8,128)(2,1)S(1)}, u32[]{:S(2)}, u32[]{:S(2)}) collective-permute-start(bf16[16,7680]{1,0:T(8,128)(2,1)S(1)} %get-tuple-element.25), channel_id=1, source_target_pairs={{0,3},{1,2},{2,1},{3,0},{4,7},{5,6},{6,5},{7,4},{8,11},{9,10},{10,... | collective-permute-start | bytes 737288 | tf_op jit(solution)/shard_map/ppermute | solution.py:25
  23.2 29.2 %collective-permute-start.7 = (bf16[16,7680]{1,0:T(8,128)(2,1)S(1)}, bf16[16,7680]{1,0:T(8,128)(2,1)S(1)}, u32[]{:S(2)}, u32[]{:S(2)}) collective-permute-start(bf16[16,7680]{1,0:T(8,128)(2,1)S(1)} %get-tuple-element.26), channel_id=1, source_target_pairs={{0,2},{1,3},{2,0},{3,1},{4,6},{5,7},{6,4},{7,5},{8,10},{9,11},{10,... | collective-permute-start | bytes 737288 | tf_op jit(solution)/shard_map/ppermute | solution.py:25
  25.3 18.2 %collective-permute-start.11 = (bf16[128,192]{1,0:T(8,128)(2,1)S(1)}, bf16[128,192]{1,0:T(8,128)(2,1)S(1)}, u32[]{:S(2)}, u32[]{:S(2)}) collective-permute-start(bf16[128,192]{1,0:T(8,128)(2,1)S(1)} %add_convert_fusion.3), channel_id=1, source_target_pairs={{0,2},{1,3},{2,0},{3,1},{4,6},{5,7},{6,4},{7,5},{8,10},{9,11},{10,... | collective-permute-start | bytes 147464 | tf_op jit(solution)/shard_map/ppermute | solution.py:25
  43.4 5.2 %collective-permute-start.12 = (bf16[128,192]{1,0:T(8,128)(2,1)S(1)}, bf16[128,192]{1,0:T(8,128)(2,1)S(1)}, u32[]{:S(2)}, u32[]{:S(2)}) collective-permute-start(bf16[128,192]{1,0:T(8,128)(2,1)S(1)} %add_convert_fusion.2), channel_id=1, source_target_pairs={{0,4},{1,5},{2,6},{3,7},{4,0},{5,1},{6,2},{7,3},{8,12},{9,13},{10,... | collective-permute-start | bytes 147464 | tf_op jit(solution)/shard_map/ppermute | solution.py:25
  48.7 13.8 %collective-permute-start.8 = (bf16[16,7680]{1,0:T(8,128)(2,1)S(1)}, bf16[16,7680]{1,0:T(8,128)(2,1)S(1)}, u32[]{:S(2)}, u32[]{:S(2)}) collective-permute-start(bf16[16,7680]{1,0:T(8,128)(2,1)S(1)} %get-tuple-element.27), channel_id=1, source_target_pairs={{0,1},{1,0},{2,3},{3,2},{4,5},{5,4},{6,7},{7,6},{8,9},{9,8},{10,11... | collective-permute-start | bytes 737288 | tf_op jit(solution)/shard_map/ppermute | solution.py:25
  50.8 13.5 %collective-permute-start.13 = (bf16[32,3840]{1,0:T(8,128)(2,1)S(1)}, bf16[32,3840]{1,0:T(8,128)(2,1)S(1)}, u32[]{:S(2)}, u32[]{:S(2)}) collective-permute-start(bf16[32,3840]{1,0:T(8,128)(2,1)S(1)} %get-tuple-element.36), channel_id=1, source_target_pairs={{0,3},{1,2},{2,1},{3,0},{4,7},{5,6},{6,5},{7,4},{8,11},{9,10},{10,... | collective-permute-start | bytes 737288 | tf_op jit(solution)/shard_map/ppermute | solution.py:25
  52.4 15.3 %collective-permute-start.15 = (bf16[32,3840]{1,0:T(8,128)(2,1)S(1)}, bf16[32,3840]{1,0:T(8,128)(2,1)S(1)}, u32[]{:S(2)}, u32[]{:S(2)}) collective-permute-start(bf16[32,3840]{1,0:T(8,128)(2,1)S(1)} %get-tuple-element.37), channel_id=1, source_target_pairs={{0,1},{1,0},{2,3},{3,2},{4,5},{5,4},{6,7},{7,6},{8,9},{9,8},{10,11... | collective-permute-start | bytes 737288 | tf_op jit(solution)/shard_map/ppermute | solution.py:25
  62.5 9.1 %collective-permute-start.14 = (bf16[32,3840]{1,0:T(8,128)(2,1)S(1)}, bf16[32,3840]{1,0:T(8,128)(2,1)S(1)}, u32[]{:S(2)}, u32[]{:S(2)}) collective-permute-start(bf16[32,3840]{1,0:T(8,128)(2,1)S(1)} %get-tuple-element.38), channel_id=1, source_target_pairs={{0,2},{1,3},{2,0},{3,1},{4,6},{5,7},{6,4},{7,5},{8,10},{9,11},{10,... | collective-permute-start | bytes 737288 | tf_op jit(solution)/shard_map/ppermute | solution.py:25
  64.3 10.0 %collective-permute-start.5 = (bf16[16,7680]{1,0:T(8,128)(2,1)S(1)}, bf16[16,7680]{1,0:T(8,128)(2,1)S(1)}, u32[]{:S(2)}, u32[]{:S(2)}) collective-permute-start(bf16[16,7680]{1,0:T(8,128)(2,1)S(1)} %get-tuple-element.23), channel_id=1, source_target_pairs={{0,1},{1,0},{2,3},{3,2},{4,5},{5,4},{6,7},{7,6},{8,9},{9,8},{10,11... | collective-permute-start | bytes 737288 | tf_op jit(solution)/shard_map/ppermute | solution.py:25
  67.7 13.0 %collective-permute-start.9 = (bf16[16,7680]{1,0:T(8,128)(2,1)S(1)}, bf16[16,7680]{1,0:T(8,128)(2,1)S(1)}, u32[]{:S(2)}, u32[]{:S(2)}) collective-permute-start(bf16[16,7680]{1,0:T(8,128)(2,1)S(1)} %add_convert_fusion), channel_id=1, source_target_pairs={{0,4},{1,5},{2,6},{3,7},{4,0},{5,1},{6,2},{7,3},{8,12},{9,13},{10,... | collective-permute-start | bytes 737288 | tf_op jit(solution)/shard_map/ppermute | solution.py:25
  71.6 9.2 %copy-start.3 = (bf16[2,64,3840]{2,1,0:T(8,128)(2,1)S(1)}, bf16[2,64,3840]{2,1,0:T(8,128)(2,1)}, u32[]{:S(2)}) copy-start(bf16[2,64,3840]{2,1,0:T(8,128)(2,1)} %param.12) | copy-start | bytes 2949124
  71.7 10.3 %collective-permute-start.16 = (bf16[16,3840]{1,0:T(8,128)(2,1)S(1)}, bf16[16,3840]{1,0:T(8,128)(2,1)S(1)}, u32[]{:S(2)}, u32[]{:S(2)}) collective-permute-start(bf16[16,3840]{1,0:T(8,128)(2,1)S(1)} %slice.362), channel_id=1, source_target_pairs={{0,4},{1,5},{2,6},{3,7},{4,0},{5,1},{6,2},{7,3},{8,12},{9,13},{10,... | collective-permute-start | bytes 368648 | tf_op jit(solution)/shard_map/ppermute | solution.py:25
  82.2 38.1 %collective-permute-start.22 = (bf16[16,11520]{1,0:T(8,128)(2,1)S(1)}, bf16[16,11520]{1,0:T(8,128)(2,1)S(1)}, u32[]{:S(2)}, u32[]{:S(2)}) collective-permute-start(bf16[16,11520]{1,0:T(8,128)(2,1)S(1)} %pad_maximum_fusion), channel_id=1, source_target_pairs={{0,3},{1,2},{2,1},{3,0},{4,7},{5,6},{6,5},{7,4},{8,11},{9,10},{10,... | collective-permute-start | bytes 1105928 | tf_op jit(solution)/shard_map/ppermute | solution.py:25
  84.5 34.6 %collective-permute-start.20 = (bf16[16,11520]{1,0:T(8,128)(2,1)S(1)}, bf16[16,11520]{1,0:T(8,128)(2,1)S(1)}, u32[]{:S(2)}, u32[]{:S(2)}) collective-permute-start(bf16[16,11520]{1,0:T(8,128)(2,1)S(1)} %pad_maximum_fusion), channel_id=1, source_target_pairs={{0,2},{1,3},{2,0},{3,1},{4,6},{5,7},{6,4},{7,5},{8,10},{9,11},{10,... | collective-permute-start | bytes 1105928 | tf_op jit(solution)/shard_map/ppermute | solution.py:25
  85.6 11.2 %collective-permute-start.18 = (bf16[16,11520]{1,0:T(8,128)(2,1)S(1)}, bf16[16,11520]{1,0:T(8,128)(2,1)S(1)}, u32[]{:S(2)}, u32[]{:S(2)}) collective-permute-start(bf16[16,11520]{1,0:T(8,128)(2,1)S(1)} %pad_maximum_fusion), channel_id=1, source_target_pairs={{0,1},{1,0},{2,3},{3,2},{4,5},{5,4},{6,7},{7,6},{8,9},{9,8},{10,11... | collective-permute-start | bytes 1105928 | tf_op jit(solution)/shard_map/ppermute | solution.py:25
  85.7 21.8 %collective-permute-start.17 = (bf16[16,11520]{1,0:T(8,128)(2,1)S(1)}, bf16[16,11520]{1,0:T(8,128)(2,1)S(1)}, u32[]{:S(2)}, u32[]{:S(2)}) collective-permute-start(bf16[16,11520]{1,0:T(8,128)(2,1)S(1)} %pad_maximum_fusion), channel_id=1, source_target_pairs={{0,4},{1,5},{2,6},{3,7},{4,0},{5,1},{6,2},{7,3},{8,12},{9,13},{10,... | collective-permute-start | bytes 1105928 | tf_op jit(solution)/shard_map/ppermute | solution.py:25
  107.6 12.8 %collective-permute-start.23 = (bf16[16,3840]{1,0:T(8,128)(2,1)S(1)}, bf16[16,3840]{1,0:T(8,128)(2,1)S(1)}, u32[]{:S(2)}, u32[]{:S(2)}) collective-permute-start(bf16[16,3840]{1,0:T(8,128)(2,1)S(1)} %get-tuple-element.43), channel_id=1, source_target_pairs={{0,3},{1,2},{2,1},{3,0},{4,7},{5,6},{6,5},{7,4},{8,11},{9,10},{10,... | collective-permute-start | bytes 368648 | tf_op jit(solution)/shard_map/ppermute | solution.py:25
  111.7 7.5 %collective-permute-start.21 = (bf16[16,3840]{1,0:T(8,128)(2,1)S(1)}, bf16[16,3840]{1,0:T(8,128)(2,1)S(1)}, u32[]{:S(2)}, u32[]{:S(2)}) collective-permute-start(bf16[16,3840]{1,0:T(8,128)(2,1)S(1)} %get-tuple-element.43), channel_id=1, source_target_pairs={{0,2},{1,3},{2,0},{3,1},{4,6},{5,7},{6,4},{7,5},{8,10},{9,11},{10,... | collective-permute-start | bytes 368648 | tf_op jit(solution)/shard_map/ppermute | solution.py:25
  111.8 4.9 %collective-permute-start.19 = (bf16[16,3840]{1,0:T(8,128)(2,1)S(1)}, bf16[16,3840]{1,0:T(8,128)(2,1)S(1)}, u32[]{:S(2)}, u32[]{:S(2)}) collective-permute-start(bf16[16,3840]{1,0:T(8,128)(2,1)S(1)} %get-tuple-element.43), channel_id=1, source_target_pairs={{0,1},{1,0},{2,3},{3,2},{4,5},{5,4},{6,7},{7,6},{8,9},{9,8},{10,11... | collective-permute-start | bytes 368648 | tf_op jit(solution)/shard_map/ppermute | solution.py:25
  112.5 17.9 %slice-start = ((s8[15728640]{0:T(1024)(128)(4,1)}), s8[4194304]{0:T(1024)(128)(4,1)S(1)}, s32[]{:S(2)}) async-start(s8[15728640]{0:T(1024)(128)(4,1)} %bitcast.53), calls=%async_computation | async-start | bytes 8388608
  116.6 12.8 %collective-permute-start.30 = (bf16[16,7680]{1,0:T(8,128)(2,1)S(1)}, bf16[16,7680]{1,0:T(8,128)(2,1)S(1)}, u32[]{:S(2)}, u32[]{:S(2)}) collective-permute-start(bf16[16,7680]{1,0:T(8,128)(2,1)S(1)} %get-tuple-element.41), channel_id=1, source_target_pairs={{0,3},{1,2},{2,1},{3,0},{4,7},{5,6},{6,5},{7,4},{8,11},{9,10},{10,... | collective-permute-start | bytes 737288 | tf_op jit(solution)/shard_map/ppermute | solution.py:25
  119.1 10.2 %collective-permute-start.29 = (bf16[16,7680]{1,0:T(8,128)(2,1)S(1)}, bf16[16,7680]{1,0:T(8,128)(2,1)S(1)}, u32[]{:S(2)}, u32[]{:S(2)}) collective-permute-start(bf16[16,7680]{1,0:T(8,128)(2,1)S(1)} %get-tuple-element.41), channel_id=1, source_target_pairs={{0,2},{1,3},{2,0},{3,1},{4,6},{5,7},{6,4},{7,5},{8,10},{9,11},{10,... | collective-permute-start | bytes 737288 | tf_op jit(solution)/shard_map/ppermute | solution.py:25
  119.2 10.1 %collective-permute-start.28 = (bf16[16,7680]{1,0:T(8,128)(2,1)S(1)}, bf16[16,7680]{1,0:T(8,128)(2,1)S(1)}, u32[]{:S(2)}, u32[]{:S(2)}) collective-permute-start(bf16[16,7680]{1,0:T(8,128)(2,1)S(1)} %get-tuple-element.41), channel_id=1, source_target_pairs={{0,1},{1,0},{2,3},{3,2},{4,5},{5,4},{6,7},{7,6},{8,9},{9,8},{10,11... | collective-permute-start | bytes 737288 | tf_op jit(solution)/shard_map/ppermute | solution.py:25
  120.4 9.9 %slice-start.1 = ((s8[15728640]{0:T(1024)(128)(4,1)}), s8[4194304]{0:T(1024)(128)(4,1)S(1)}, s32[]{:S(2)}) async-start(s8[15728640]{0:T(1024)(128)(4,1)} %bitcast.53), calls=%async_computation.1 | async-start | bytes 8388608
  120.4 9.9 %slice-start.2 = ((s8[15728640]{0:T(1024)(128)(4,1)}), s8[4194304]{0:T(1024)(128)(4,1)S(1)}, s32[]{:S(2)}) async-start(s8[15728640]{0:T(1024)(128)(4,1)} %bitcast.53), calls=%async_computation.2 | async-start | bytes 8388608
  122.1 1.3 collective-permute-start.26
  123.4 7.0 %slice-start.3 = ((s8[15728640]{0:T(1024)(128)(4,1)}), s8[3145728]{0:T(1024)(128)(4,1)S(1)}, s32[]{:S(2)}) async-start(s8[15728640]{0:T(1024)(128)(4,1)} %bitcast.53), calls=%async_computation.3 | async-start | bytes 6291456
  123.4 3.8 %collective-permute-start.27 = (bf16[128,64]{0,1:T(8,128)(2,1)S(1)}, bf16[128,64]{0,1:T(8,128)(2,1)S(1)}, u32[]{:S(2)}, u32[]{:S(2)}) collective-permute-start(bf16[128,64]{0,1:T(8,128)(2,1)S(1)} %add_convert_fusion.7), channel_id=1, source_target_pairs={{0,16},{8,24},{16,0},{24,8},{1,17},{9,25},{17,1},{25,9},{2,18},{10... | collective-permute-start | bytes 49160 | tf_op jit(solution)/shard_map/ppermute | solution.py:25
  125.5 15.1 %collective-permute-start.24 = (bf16[64,1024]{1,0:T(8,128)(2,1)S(1)}, bf16[64,1024]{1,0:T(8,128)(2,1)S(1)}, u32[]{:S(2)}, u32[]{:S(2)}) collective-permute-start(bf16[64,1024]{1,0:T(8,128)(2,1)S(1)} %slice.361), channel_id=1, source_target_pairs={{0,8},{8,0},{16,24},{24,16},{1,9},{9,1},{17,25},{25,17},{2,10},{10... | collective-permute-start | bytes 393224 | tf_op jit(solution)/shard_map/ppermute | solution.py:25
  133.7 5.2 %collective-permute-start.33 = (bf16[128,128]{0,1:T(8,128)(2,1)S(1)}, bf16[128,128]{0,1:T(8,128)(2,1)S(1)}, u32[]{:S(2)}, u32[]{:S(2)}) collective-permute-start(bf16[128,128]{0,1:T(8,128)(2,1)S(1)} %pad_maximum_fusion.1), channel_id=1, source_target_pairs={{0,8},{8,0},{16,24},{24,16},{1,9},{9,1},{17,25},{25,17},{2,10},{10... | collective-permute-start | bytes 98312 | tf_op jit(solution)/shard_map/ppermute | solution.py:25
  136.9 7.7 %collective-permute-start.31 = (bf16[64,1024]{1,0:T(8,128)(2,1)S(1)}, bf16[64,1024]{1,0:T(8,128)(2,1)S(1)}, u32[]{:S(2)}, u32[]{:S(2)}) collective-permute-start(bf16[64,1024]{1,0:T(8,128)(2,1)S(1)} %slice.360), channel_id=1, source_target_pairs={{0,8},{8,0},{16,24},{24,16},{1,9},{9,1},{17,25},{25,17},{2,10},{10... | collective-permute-start | bytes 393224 | tf_op jit(solution)/shard_map/ppermute | solution.py:25
  138.9 4.0 %collective-permute-start.34 = (bf16[128,128]{0,1:T(8,128)(2,1)S(1)}, bf16[128,128]{0,1:T(8,128)(2,1)S(1)}, u32[]{:S(2)}, u32[]{:S(2)}) collective-permute-start(bf16[128,128]{0,1:T(8,128)(2,1)S(1)} %add_convert_fusion.6), channel_id=1, source_target_pairs={{0,16},{8,24},{16,0},{24,8},{1,17},{9,25},{17,1},{25,9},{2,18},{10... | collective-permute-start | bytes 98312 | tf_op jit(solution)/shard_map/ppermute | solution.py:25
  140.6 5.8 %collective-permute-start.25 = (bf16[32,1024]{1,0:T(8,128)(2,1)S(1)}, bf16[32,1024]{1,0:T(8,128)(2,1)S(1)}, u32[]{:S(2)}, u32[]{:S(2)}) collective-permute-start(bf16[32,1024]{1,0:T(8,128)(2,1)S(1)} %slice.364), channel_id=1, source_target_pairs={{0,16},{8,24},{16,0},{24,8},{1,17},{9,25},{17,1},{25,9},{2,18},{10... | collective-permute-start | bytes 196616 | tf_op jit(solution)/shard_map/ppermute | solution.py:25
  144.7 4.3 %collective-permute-start.32 = (bf16[32,1024]{1,0:T(8,128)(2,1)S(1)}, bf16[32,1024]{1,0:T(8,128)(2,1)S(1)}, u32[]{:S(2)}, u32[]{:S(2)}) collective-permute-start(bf16[32,1024]{1,0:T(8,128)(2,1)S(1)} %slice.363), channel_id=1, source_target_pairs={{0,16},{8,24},{16,0},{24,8},{1,17},{9,25},{17,1},{25,9},{2,18},{10... | collective-permute-start | bytes 196616 | tf_op jit(solution)/shard_map/ppermute | solution.py:25
